TPU v7x, 32 devices: a whole 2x2x4 slice. The times are simulated.
32 devices in a mesh: dp: 32 (over z, y, x, core).
Axes of the slice: x: 2, y: 2, z: 4, core: 2. Of those that a mesh axis runs over, the one named last changes fastest.
Arguments:
- query_features: bfloat16 [8192, 768], P('dp'), may hold values from -24 to 24
- passage_features: bfloat16 [8192, 768], P('dp'), may hold values from -24 to 24
- counts: int32 [32], replicated, may hold values from 128 to 256, as said below
- positives: int32 [8192], P('dp'), may hold values from 0 to 4351
- w_first: bfloat16 [768, 1536], replicated, may hold values from -0.21875 to 0.21875
- w_second: bfloat16 [1536, 384], replicated, may hold values from -0.15625 to 0.15625
Outputs:
- mean_loss: float32 [], replicated
- grad_first: float32 [768, 1536], P(None, 'dp')
- grad_second: float32 [1536, 384], P('dp')
Inputs may be any that keep to these rules, and one draw needn't show every extreme that they name: Device i holds counts[i] pairs in the first slots of its 256 slots. Each entry is 128 or 256; among the 16 devices whose indices agree modulo 32 // 16 exactly one entry is 256, so the entries sum to 4352. `positives`: only entries of occupied slots are used; an entry is the index of a passage in the order of occupied slots, device by device.
All inputs are finite; a program needn't handle non-finite values.
Results may differ from a plain program's by a relative error of at most 0.0043.
The roundings to bfloat16 on the way count: a program that leaves them out, or rounds other values in their place, can miss the bound.
Values may be sent and summed in bfloat16 or wider, within the bound.
A program may use at most 128 MiB of HBM per device.

v0:
```python
import jax
import jax.numpy as jnp
from jax import lax
from jax.sharding import PartitionSpec as P


def from_partner(block, axis, apart):
    count = lax.axis_size(axis)
    route = []
    for low in range(count):
        high = low | 1 << apart
        if high != low and high < count:
            route += [(low, high), (high, low)]
    return lax.ppermute(block, axis, route)


def gelu_tanh(values):
    return jax.nn.gelu(values, approximate=True)


def tower_pass(features, w_first, w_second):
    pre_act = jnp.dot(features, w_first, preferred_element_type=jnp.float32)
    hidden = gelu_tanh(pre_act).astype(jnp.bfloat16)
    embedded = jnp.dot(hidden, w_second, preferred_element_type=jnp.float32).astype(jnp.bfloat16)
    return (pre_act, hidden, embedded)


def weight_terms(features, pre_act, hidden, grads, w_second):
    grad_second = lax.dot_general(
        hidden, grads, (((0,), (0,)), ((), ())), preferred_element_type=jnp.float32
    )
    back_act = lax.dot_general(
        grads, w_second, (((1,), (1,)), ((), ())), preferred_element_type=jnp.float32
    )
    pull_back = jax.vjp(gelu_tanh, pre_act)[1]
    pre_grad = pull_back(back_act)[0].astype(jnp.bfloat16)
    grad_first = lax.dot_general(
        features, pre_grad, (((0,), (0,)), ((), ())), preferred_element_type=jnp.float32
    )
    return (grad_first, grad_second)


def body(query_features, passage_features, counts, positives, w_first, w_second):
    device_count = lax.axis_size("dp")
    my_index = lax.axis_index("dp")
    stride = device_count // 16
    high_bits = stride.bit_length() - 1
    capacity = query_features.shape[0]
    base_rows = capacity // 2
    unit_rows = base_rows // 16
    block_rows = base_rows + unit_rows
    spare_units = 15
    pair_count = block_rows * device_count
    score_scale = 2.5 * w_second.shape[1] ** (-0.5)
    devices = jnp.arange(device_count, dtype=jnp.int32)
    group_of = devices % stride
    group_place = devices // stride
    heavy_dev = (counts > base_rows).astype(jnp.int32)
    light_dev = 1 - heavy_dev
    same_mat = group_of[:, None] == group_of[None, :]
    earlier = same_mat & (group_place[None, :] < group_place[:, None]) & (light_dev[None, :] == 1)
    piece_slot = jnp.sum(earlier.astype(jnp.int32), axis=1)
    source = jnp.sum(jnp.where(same_mat & (heavy_dev[None, :] == 1), devices[None, :], 0), axis=1)
    my_heavy = jnp.sum(jnp.where(devices == my_index, heavy_dev, 0))
    my_group = my_index % stride
    group_pos = my_index // stride
    same_group = group_of == my_group
    heavy_pos = jnp.sum(jnp.where(same_group & (heavy_dev == 1), group_place, 0))
    relative = jnp.bitwise_xor(group_pos, heavy_pos)
    slot_ids = jnp.arange(16, dtype=jnp.int32)
    slot_dest = my_group + jnp.bitwise_xor(heavy_pos, slot_ids) * stride
    slot_piece = jnp.take(piece_slot, slot_dest)

    def keep_tail(row_data, arrived):
        tail_rows = jnp.where(my_heavy == 1, row_data[base_rows:block_rows], arrived)
        return jnp.concatenate([row_data[:base_rows], tail_rows], axis=0)

    all_pos = lax.all_gather(positives, "dp", axis=0, tiled=True)
    within = jnp.arange(block_rows, dtype=jnp.int32)
    moved_rows = (within[None, :] >= base_rows) & (heavy_dev[:, None] == 0)
    slot_grid = jnp.where(
        moved_rows,
        source[:, None] * capacity
        + block_rows
        + piece_slot[:, None] * unit_rows
        + (within[None, :] - base_rows),
        devices[:, None] * capacity + within[None, :],
    ).reshape(-1)
    anchor = jnp.take(all_pos, slot_grid)
    offsets = jnp.cumsum(counts) - counts
    inside = (offsets[None, :] <= anchor[:, None]) & (anchor[:, None] < (offsets + counts)[None, :])
    owner_dev = jnp.sum(jnp.where(inside, devices[None, :], 0), axis=1)
    owner_start = jnp.sum(jnp.where(inside, offsets[None, :], 0), axis=1)
    owner_group = owner_dev % stride
    offset_row = anchor - owner_start
    beyond = jnp.maximum(offset_row - block_rows, 0)
    unit_ids = beyond // unit_rows
    target_hit = (
        (light_dev[None, :] == 1)
        & (group_of[None, :] == owner_group[:, None])
        & (piece_slot[None, :] == unit_ids[:, None])
    )
    target = jnp.sum(jnp.where(target_hit, devices[None, :], 0), axis=1)
    new_pos = jnp.where(
        offset_row < block_rows,
        owner_dev * block_rows + offset_row,
        target * block_rows + base_rows + beyond % unit_rows,
    )
    stacked = jnp.stack((query_features, passage_features))
    width = stacked.shape[2]
    overflow = stacked[:, block_rows:].reshape(2, spare_units, unit_rows, width)
    held = jnp.take(overflow, slot_piece, axis=1)
    held = jnp.where((slot_ids > 0)[None, :, None, None], held, jnp.zeros((), held.dtype))
    for bit in range(4):
        halves = held.reshape(2, held.shape[1] // 2, 2, unit_rows, width)
        arrived = from_partner(halves[:, :, 1], "dp", high_bits + bit)
        taker = jnp.bitwise_and(jnp.right_shift(relative, bit), 1) == 1
        held = jnp.where(taker, arrived, halves[:, :, 0])
    arrived_rows = held[:, 0]
    rows_query = keep_tail(query_features, arrived_rows[0])
    rows_passage = keep_tail(passage_features, arrived_rows[1])
    pre_query, hidden_query, emb_query = tower_pass(rows_query, w_first, w_second)
    pre_passage, hidden_passage, emb_passage = tower_pass(rows_passage, w_first, w_second)
    all_queries, all_passages = (
        lax.all_gather(emb_query, "dp", axis=0, tiled=True),
        lax.all_gather(emb_passage, "dp", axis=0, tiled=True),
    )
    columns = jnp.arange(pair_count, dtype=jnp.int32)
    own_pos = lax.dynamic_slice_in_dim(new_pos, my_index * block_rows, block_rows, 0)
    scores = (
        lax.dot_general(
            emb_query, all_passages, (((1,), (1,)), ((), ())), preferred_element_type=jnp.float32
        )
        * score_scale
    )
    row_top = jnp.max(scores, axis=1)
    log_norm = row_top + jnp.log(jnp.sum(jnp.exp(scores - row_top[:, None]), axis=1))
    is_positive = own_pos[:, None] == columns[None, :]
    pos_score = jnp.sum(jnp.where(is_positive, scores, jnp.zeros_like(scores)), axis=1)
    weights = (jnp.exp(scores - log_norm[:, None]) - is_positive.astype(jnp.float32)).astype(
        jnp.bfloat16
    )
    query_grads = (
        score_scale * jnp.dot(weights, all_passages, preferred_element_type=jnp.float32)
    ).astype(jnp.bfloat16)
    all_norm, all_score = (
        lax.all_gather(log_norm, "dp", axis=0, tiled=True),
        lax.all_gather(pos_score, "dp", axis=0, tiled=True),
    )
    mean_loss = jnp.sum(all_norm - all_score) / pair_count
    own_columns = my_index * block_rows + within
    scores_back = (
        lax.dot_general(
            emb_passage, all_queries, (((1,), (1,)), ((), ())), preferred_element_type=jnp.float32
        )
        * score_scale
    )
    is_target = new_pos[None, :] == own_columns[:, None]
    weights_back = (
        jnp.exp(scores_back - all_norm[None, :]) - is_target.astype(jnp.float32)
    ).astype(jnp.bfloat16)
    passage_grads = (
        score_scale * jnp.dot(weights_back, all_queries, preferred_element_type=jnp.float32)
    ).astype(jnp.bfloat16)
    act_query, hid_query, unused_query = tower_pass(rows_query, w_first, w_second)
    act_passage, hid_passage, unused_passage = tower_pass(rows_passage, w_first, w_second)
    first_query, second_query = weight_terms(
        rows_query, act_query, hid_query, query_grads, w_second
    )
    first_passage, second_passage = weight_terms(
        rows_passage, act_passage, hid_passage, passage_grads, w_second
    )
    grad_first, grad_second = (
        lax.psum_scatter(first_query + first_passage, "dp", scatter_dimension=1, tiled=True),
        lax.psum_scatter(second_query + second_passage, "dp", scatter_dimension=0, tiled=True),
    )
    return (mean_loss, grad_first, grad_second)


def solution(mesh):
    return jax.shard_map(
        body,
        mesh=mesh,
        in_specs=(P("dp", None), P("dp", None), P(), P("dp"), P(), P()),
        out_specs=(P(), P(None, "dp"), P("dp", None)),
        check_vma=False,
    )
```

profile of v0, /device:TPU:9, one launch (start us, length us, event | category | flops | bytes accessed | tf_op | source)
XLA Modules:
  0.0 403.3 jit_solution(9347207216545790159)
XLA Ops:
  7.3 0.8 broadcast_compare_fusion.1
  8.1 0.7 copy.51
  9.0 1.9 fusion.59
  10.9 0.7 fusion.62
  11.7 0.7 gather_fusion
  12.4 0.7 fusion.60
  13.1 1.0 fusion.39
  14.2 0.6 gather_fusion.1
  14.8 0.7 fusion.55
  15.6 1.3 collective-permute-start
  17.5 3.9 collective-permute-done
  21.5 1.3 collective-permute-start.1
  22.8 2.2 collective-permute-done.1
  25.3 2.7 collective-permute-done.2
  28.1 2.4 collective-permute-start.3
  30.5 0.9 slice.59
  32.1 0.7 fusion.53
  32.8 0.5 fusion.41
  33.3 2.4 convolution_convert_fusion
  35.8 1.0 slice.47
  36.8 0.7 fusion.54
  37.6 0.5 fusion.42
  38.1 0.9 copy-done.2
  39.0 1.1 convolution_convert_fusion.1
  40.5 0.7 select_n.314
  41.2 40.1 %all-gather = s32[32,1,256]{2,1,0:T(1,128)S(1)} all-gather(s32[1,1,256]{2,1,0:T(1,128)S(1)} %bitcast.91), channel_id=1, replica_groups=mesh['dp'=32] {'dp'}, dimensions={0}, use_global_device_ids=true | all-gather | bytes 33792 | tf_op jit(solution)/shard_map/all_gather | solution.py:78
  81.3 0.6 pad_clamp_fusion
  82.0 32.5 %gather_fusion.2 = s32[4352]{0:T(1024)} fusion(s32[8192]{0:T(1024)S(1)} %bitcast.80, s32[5120]{0:T(1024)} %pad_clamp_fusion), kind=kCustom, calls=%fused_computation.2 | custom fusion | bytes 52224 | tf_op jit(solution)/shard_map/jit(_take)/gather | solution.py:89
  114.4 0.8 and_select_fusion
  115.2 0.9 select_reduce_fusion.2
  116.2 0.9 select_reduce_fusion.1
  117.1 0.6 copy-done.10
  117.8 3.6 fusion.82
  121.5 1.5 copy-done.1
  123.0 0.8 select_reduce_fusion
  124.2 45.3 %all-reduce.2 = (f32[4352]{0:T(1024)}, f32[4352]{0:T(1024)}) all-reduce(f32[4352]{0:T(1024)S(1)} %get-tuple-element.13, f32[4352]{0:T(1024)S(1)} %dynamic-update-slice.1), channel_id=1, replica_groups=mesh['dp'=32] {'dp'}, use_global_device_ids=true, to_apply=%add | all-reduce | flops 8704 | bytes 69632
  169.4 3.6 fusion.9
  173.1 0.6 copy-done.7
  173.7 2.1 fusion.80
  175.8 5.2 %fusion.8 = bf16[136,384]{1,0:T(8,128)(2,1)S(1)} fusion(bf16[4352,384]{1,0:T(8,128)(2,1)} %all-gather.6.cloned.1.call-done, bf16[136,384]{1,0:T(8,128)(2,1)} %convolution_convert_fusion, s32[4352]{0:T(1024)S(1)} %copy-done.11, f32[4352]{0:T(1024)} %get-tuple-element.11, s32[136]{0:T(256)S(1)} %iota_add_fusion), kind=kOutput, calls=%fused_computation.24 | convolution fusion | flops 912771072 | bytes 3586592 | tf_op jit(solution)/shard_map/dot_general | solution.py:163
  181.1 3.8 convolution_add_fusion.1
  185.1 0.5 copy-done.9
  185.6 5.4 %fusion.25 = f32[768,1536]{0,1:T(8,128)} fusion(f32[136,1536]{1,0:T(8,128)} %copy-done.2, bf16[8,768]{1,0:T(8,128)(2,1)S(1)} %copy-done.9, bf16[128,768]{1,0:T(8,128)(2,1)} %copy-done.5, bf16[136,384]{1,0:T(8,128)(2,1)} %copy-done.7, bf16[1536,384]{1,0:T(8,128)(2,1)} %param.11), kind=kOutput, calls=%fused_computation.48 | convolution fusion | flops 485892096 | bytes 7047168 | tf_op jit(solution)/shard_map/dot_general | solution.py:37
  191.0 6.5 %convolution_add_fusion = f32[768,1536]{0,1:T(8,128)} fusion(f32[768,1536]{0,1:T(8,128)} %fusion.25, f32[136,1536]{1,0:T(8,128)S(1)} %fusion.41, bf16[8,768]{1,0:T(8,128)(2,1)S(1)} %fusion.53, bf16[128,768]{1,0:T(8,128)(2,1)S(1)} %slice.59, bf16[136,384]{1,0:T(8,128)(2,1)S(1)} %fusion.8, bf16[1536,384]{1,0:T(8,128)(2,1)} %param.11), kind=kOutput, calls=%fused_computation.9 | convolution fusion | flops 487071744 | bytes 11765760 | tf_op jit(solution)/shard_map/dot_general | solution.py:37
  197.5 0.7 copy-done.12
  198.3 0.6 subtract_reduce_fusion
  199.5 83.5 %reduce-scatter.5.cloned.1.call-done = f32[48,384]{1,0:T(8,128)} async-done(((f32[1536,384]{1,0:T(8,128)}), f32[48,384]{1,0:T(8,128)}) %reduce-scatter.5.cloned.1.call-update) | async-done | bytes 73744 | tf_op jit(solution)/shard_map/reduce_scatter | solution.py:175
  283.0 112.6 %reduce-scatter.3.cloned.1.call-done = f32[768,48]{0,1:T(8,128)} async-done(((f32[768,1536]{0,1:T(8,128)}), f32[768,48]{0,1:T(8,128)}) %reduce-scatter.3.cloned.1.call-update) | async-done | bytes 147472 | tf_op jit(solution)/shard_map/reduce_scatter | solution.py:174
  (71 shorter events, 2.2 us)
Async XLA Ops:
  7.2 25.7 %copy-start = (bf16[768,1536]{1,0:T(8,128)(2,1)S(1)}, bf16[768,1536]{1,0:T(8,128)(2,1)}, u32[]{:S(2)}) copy-start(bf16[768,1536]{1,0:T(8,128)(2,1)} %param.10) | copy-start | bytes 7077892
  7.2 110.6 %all-gather.4.cloned.1.call-start = ((), (), s32[]{:S(2)}) async-start(), calls=%async_computation.2 | async-start | bytes 3446784 | tf_op jit(solution)/shard_map/all_gather | solution.py:126
  8.1 5.1 %copy-start.14 = (pred[32]{0:T(512)(128)(4,1)}, pred[32]{0:T(512)(128)(4,1)S(1)}, u32[]{:S(2)}) copy-start(pred[32]{0:T(512)(128)(4,1)S(1)} %get-tuple-element.18) | copy-start | bytes 100
  15.6 5.9 %collective-permute-start = (bf16[2,8,8,768]{3,2,1,0:T(8,128)(2,1)S(1)}, bf16[2,8,8,768]{3,2,1,0:T(8,128)(2,1)S(1)}, u32[]{:S(2)}, u32[]{:S(2)}) collective-permute-start(bf16[2,8,8,768]{3,2,1,0:T(8,128)(2,1)S(1)} %slice_bitcast_fusion.1), channel_id=1, source_target_pairs={{0,2},{2,0},{1,3},{3,1},{4,6},{6,4},{5,7},{7,5},{8,10},{10,8},{9,1... | collective-permute-start | bytes 589832 | tf_op jit(solution)/shard_map/ppermute | solution.py:14
  21.5 3.5 collective-permute-start.1
  25.1 3.0 collective-permute-start.2
  28.1 4.0 collective-permute-start.3
  35.7 140.1 %all-gather.6.cloned.1.call-start = ((), (), s32[]{:S(2)}) async-start(), calls=%async_computation.3 | async-start | bytes 3446784 | tf_op jit(solution)/shard_map/all_gather | solution.py:125
  35.8 3.3 copy-start.4
  36.8 0.8 copy-start.5
  37.6 2.6 copy-start.8
  38.1 1.0 copy-start.2
  39.0 2.1 copy-start.15
  40.2 242.8 %reduce-scatter.5.cloned.1.call-start = ((), (), s32[]{:S(2)}) async-start(), calls=%async_computation.5 | async-start | bytes 2433024 | tf_op jit(solution)/shard_map/reduce_scatter | solution.py:175
  82.0 35.9 %copy-start.6 = (bf16[136,384]{1,0:T(8,128)(2,1)S(1)}, bf16[136,384]{1,0:T(8,128)(2,1)}, u32[]{:S(2)}) copy-start(bf16[136,384]{1,0:T(8,128)(2,1)} %convolution_convert_fusion.1) | copy-start | bytes 313348
  117.1 0.6 copy-start.10
  121.5 1.5 copy-start.1
  169.4 4.3 %copy-start.3 = (f32[136,1536]{1,0:T(8,128)S(1)}, f32[136,1536]{1,0:T(8,128)}, u32[]{:S(2)}) copy-start(f32[136,1536]{1,0:T(8,128)} %copy-done.2) | copy-start | bytes 2506756
  173.1 0.6 copy-start.7
  173.7 2.1 copy-start.11
  184.9 0.7 copy-start.9
  184.9 210.7 %reduce-scatter.3.cloned.1.call-start = ((), (), s32[]{:S(2)}) async-start(), calls=%async_computation.4 | async-start | bytes 4866048 | tf_op jit(solution)/shard_map/reduce_scatter | solution.py:174
  197.5 0.7 copy-start.12
  197.5 0.7 copy-start.13
Sparse Core Ops, SparseCore 0:
  35.9 64.3 all-gather.3
  103.6 58.8 all-gather.5
  185.0 97.9 reduce-scatter.4
  288.9 106.6 reduce-scatter.2
where the time goes:
time: 408 us; the launch traced here: 403 us
  waiting for transfers between devices  205 us (50%)
  blocking collectives  85.3 us (21%)
  local copies, waits for them, and re-layouts  42.6 us (10%)
  matrix products  34.8 us (9%)
  between operations  17.2 us (4%)
  other arithmetic  12.7 us (3%)
  starting transfers between devices  5.57 us (1%)
    reduce_scatter x1, waiting for transfers between devices, body(): lax.psum_scatter(first_query + first_passage, 'dp', scatter_dimension=1,...  113 us
    reduce_scatter x1, waiting for transfers between devices, body(): lax.psum_scatter(second_query + second_passage, 'dp', scatter_dimension=0...  83.5 us
    unnamed x1, blocking collectives  45.3 us
    all_gather x1, blocking collectives, body(): all_pos = lax.all_gather(positives, 'dp', axis=0, tiled=True)  40.1 us
    gather x1, local copies, waits for them, and re-layouts, body(): anchor = jnp.take(all_pos, slot_grid)  32.5 us
    dot_general x2, matrix products, weight_terms(): lax.dot_general(features, pre_grad, (((0,), (0,)), ((), ())), preferred_e...  11.9 us
    ppermute x4, waiting for transfers between devices, from_partner(): return lax.ppermute(block, axis, route)  8.89 us
  transfers between devices with their start and end apart: 8, of which 5 were waited for; matrix products, arithmetic and copies ran while one was open for 16% of the time, Pallas kernels for 0%

commit v1 on v0

v1 whole, which is shorter than its diff:
```python
import functools

import jax
import jax.numpy as jnp
from jax import lax
from jax.experimental import pallas as pl
from jax.experimental.pallas import tpu as pltpu
from jax.sharding import PartitionSpec as P

MESH = pl.DeviceIdType.MESH
F32 = jnp.float32
BF16 = jnp.bfloat16


def gelu_tanh(values):
    return jax.nn.gelu(values, approximate=True)


def place_of(group, me, size, plane):
    count = size // plane
    if group == "plane":
        place = lax.rem(me, plane)
        return place, plane, 1, me - place
    if group == "line":
        return lax.div(me, plane), count, plane, lax.rem(me, plane)
    if group == "pair":
        place = lax.rem(me, 2)
        return place, 2, 1, me - place
    if group == "lane":
        place = lax.div(lax.rem(me, plane), 2)
        return place, plane // 2, 2, me - 2 * place
    stride = size // 16
    return lax.div(me, stride), 16, stride, lax.rem(me, stride)


def members_of(group, size, plane):
    return {"plane": plane, "line": size // plane, "pair": 2, "lane": plane // 2, "units": 16}[group]


def exchange_kernel(size, plane, plan, *refs):
    count = len(plan)
    sources, landings = refs[:count], refs[count : 2 * count]
    send_sem, recv_sem, own_sem = refs[2 * count :]
    me = lax.axis_index("dp")
    barrier = pltpu.get_barrier_semaphore()
    greeted = 0
    for group in sorted({group for group, _ in plan}):
        place, members, step, first = place_of(group, me, size, plane)
        for k in range(1, members):
            other = first + step * lax.rem(place + k, members)
            pl.semaphore_signal(barrier, inc=1, device_id=(other,), device_id_type=MESH)
            greeted += 1
    pl.semaphore_wait(barrier, greeted)
    copies = []
    used = 0
    for item, (group, kind) in enumerate(plan):
        place, members, step, first = place_of(group, me, size, plane)
        source, landing = sources[item], landings[item]
        for k in range(1, members):
            wrap = lax.div(place + k, members)
            there = place + k - members * wrap
            if kind == "gather":
                part = source
            elif kind == "scatter":
                part = source.at[there]
            elif kind == "column":
                part = source.at[:, there]
            else:
                part = source.at[there - 1 + wrap]
            copy = pltpu.make_async_remote_copy(
                src_ref=part,
                dst_ref=landing.at[place],
                send_sem=send_sem.at[used],
                recv_sem=recv_sem.at[used],
                device_id=(first + step * there,),
                device_id_type=MESH,
            )
            copy.start()
            copies.append(copy)
            used += 1
        if kind == "gather":
            own = pltpu.make_async_copy(source, landing.at[place], own_sem.at[item])
            own.start()
            copies.append(own)
    for copy in copies:
        copy.wait()


def exchange(name, size, plane, *items):
    plan = tuple((group, kind) for group, kind, _ in items)
    arrays = [array for _, _, array in items]
    shapes = []
    total = 0
    for group, kind, array in items:
        members = members_of(group, size, plane)
        total += members - 1
        if kind == "gather":
            block = array.shape
        elif kind == "column":
            block = array.shape[:1] + array.shape[2:]
        else:
            block = array.shape[1:]
        shapes.append(jax.ShapeDtypeStruct((members,) + block, array.dtype))
    return pl.pallas_call(
        functools.partial(exchange_kernel, size, plane, plan),
        out_shape=shapes,
        in_specs=[
            pl.BlockSpec(memory_space=pltpu.VMEM if kind == "gather" else pl.ANY) for _, kind in plan
        ],
        out_specs=[pl.BlockSpec(memory_space=pl.ANY)] * len(items),
        scratch_shapes=[
            pltpu.SemaphoreType.DMA((total,)),
            pltpu.SemaphoreType.DMA((total,)),
            pltpu.SemaphoreType.DMA((len(items),)),
        ],
        compiler_params=pltpu.CompilerParams(collective_id=name, has_side_effects=True),
    )(*arrays)


def last_kernel(size, plane, source, landing, send_sem, recv_sem):
    me = lax.axis_index("dp")
    rows = size // plane
    half = rows // 2
    row = lax.div(me, plane)
    core = lax.rem(me, 2)
    column = lax.rem(me, plane) - core
    barrier = pltpu.get_barrier_semaphore()
    spot = 2 * row + core
    for k in range(1, 2 * rows):
        other = lax.rem(spot + k, 2 * rows)
        index = plane * lax.div(other, 2) + column + lax.rem(other, 2)
        pl.semaphore_signal(barrier, inc=1, device_id=(index,), device_id_type=MESH)
    pl.semaphore_wait(barrier, 2 * rows - 1)
    sender_core = lax.div(row, half)

    def copy_of(i, j):
        return pltpu.make_async_remote_copy(
            src_ref=source.at[i, j],
            dst_ref=landing.at[row],
            send_sem=send_sem.at[i, j],
            recv_sem=recv_sem.at[row],
            device_id=(plane * (half * core + i) + column + j,),
            device_id_type=MESH,
        )

    for i in range(half):
        for j in range(2):
            target = plane * (half * core + i) + column + j

            @pl.when(target != me)
            def _():
                copy_of(i, j).start()

    for i in range(half):
        for j in range(2):
            target = plane * (half * core + i) + column + j

            @pl.when(target != me)
            def _():
                copy_of(i, j).wait_send()

    for sender_row in range(rows):
        sender = plane * sender_row + column + sender_core

        @pl.when(sender != me)
        def _():
            pltpu.make_async_remote_copy(
                src_ref=source.at[0, 0],
                dst_ref=landing.at[sender_row],
                send_sem=send_sem.at[0, 0],
                recv_sem=recv_sem.at[sender_row],
                device_id=(sender,),
                device_id_type=MESH,
            ).wait_recv()


def last_exchange(name, size, plane, chunks):
    rows = size // plane
    return pl.pallas_call(
        functools.partial(last_kernel, size, plane),
        out_shape=jax.ShapeDtypeStruct((rows,) + chunks.shape[2:], chunks.dtype),
        in_specs=[pl.BlockSpec(memory_space=pl.ANY)],
        out_specs=pl.BlockSpec(memory_space=pl.ANY),
        scratch_shapes=[
            pltpu.SemaphoreType.DMA((rows // 2, 2)),
            pltpu.SemaphoreType.DMA((rows,)),
        ],
        compiler_params=pltpu.CompilerParams(collective_id=name, has_side_effects=True),
    )(chunks)


def sum_with_own(own, arrived, place):
    slots = jnp.arange(arrived.shape[0], dtype=jnp.int32)
    mine = (slots == place).reshape((-1,) + (1,) * (arrived.ndim - 1))
    return jnp.sum(jnp.where(mine, own, arrived.astype(F32)), axis=0)


def body(query_features, passage_features, counts, positives, w_first, w_second):
    device_count = lax.axis_size("dp")
    plane = 1 << device_count.bit_length() // 2
    rows_of_planes = device_count // plane
    my_index = lax.axis_index("dp")
    stride = device_count // 16
    capacity, width = query_features.shape
    hidden_width, embed = w_second.shape
    base_rows = capacity // 2
    unit_rows = base_rows // 16
    block_rows = base_rows + unit_rows
    pair_count = block_rows * device_count
    score_scale = 2.5 * embed ** (-0.5)

    devices = jnp.arange(device_count, dtype=jnp.int32)
    group_of = devices % stride
    group_place = devices // stride
    heavy_dev = (counts > base_rows).astype(jnp.int32)
    same_mat = group_of[:, None] == group_of[None, :]
    heavy_place = jnp.sum(jnp.where(same_mat, (heavy_dev * group_place)[None, :], 0), axis=1)
    my_heavy = jnp.sum(jnp.where(devices == my_index, heavy_dev, 0))
    heavy_pos = jnp.sum(jnp.where(devices == my_index, heavy_place, 0))

    earlier_dev = devices[None, :] < devices[:, None]
    offsets = jnp.sum(jnp.where(earlier_dev, counts[None, :], 0), axis=1)
    inside = (offsets[None, :] <= positives[:, None]) & (
        positives[:, None] < (offsets + counts)[None, :]
    )
    owner_dev = jnp.sum(jnp.where(inside, devices[None, :], 0), axis=1)
    offset_row = positives - jnp.sum(jnp.where(inside, offsets[None, :], 0), axis=1)
    owner_heavy = jnp.sum(jnp.where(inside, heavy_place[None, :], 0), axis=1)
    beyond = jnp.maximum(offset_row - block_rows, 0)
    unit_ids = beyond // unit_rows
    target_place = unit_ids + (unit_ids >= owner_heavy).astype(jnp.int32)
    target = target_place * stride + owner_dev % stride
    new_pos = jnp.where(
        offset_row < block_rows,
        owner_dev * block_rows + offset_row,
        target * block_rows + base_rows + beyond % unit_rows,
    )
    lanes = jnp.arange(128, dtype=jnp.int32)
    coded = jnp.where(lanes[None, :] == 0, new_pos[:, None] // 256, new_pos[:, None] % 256)
    coded = jnp.where(lanes[None, :] < 2, coded, 0).astype(BF16)

    packed = jnp.concatenate([query_features, passage_features, coded], axis=1)
    units = packed[block_rows:].reshape(15, unit_rows, packed.shape[1])
    (arrived,) = exchange(0, device_count, plane, ("units", "unit", units))
    tail = lax.dynamic_index_in_dim(arrived, heavy_pos, 0, keepdims=False)
    tail = jnp.where(my_heavy == 1, packed[base_rows:block_rows], tail)
    tail_pos = (
        tail[:, 2 * width].astype(jnp.int32) * 256 + tail[:, 2 * width + 1].astype(jnp.int32)
    )
    own_pos = jnp.concatenate([new_pos[:base_rows], tail_pos])
    features = jnp.concatenate(
        [
            query_features[:base_rows],
            tail[:, :width],
            passage_features[:base_rows],
            tail[:, width : 2 * width],
        ],
        axis=0,
    )

    pre_act = jnp.dot(features, w_first, preferred_element_type=F32)
    hidden = gelu_tanh(pre_act).astype(BF16)
    embedded = jnp.dot(hidden, w_second, preferred_element_type=F32).astype(BF16)
    pos_tile = jnp.pad(own_pos, (0, 1024 - block_rows)).reshape(8, 128)
    queries, all_pos, passages, pair_features = exchange(
        1,
        device_count,
        plane,
        ("plane", "gather", embedded[:block_rows]),
        ("plane", "gather", pos_tile),
        ("line", "gather", embedded[block_rows:]),
        ("pair", "gather", features),
    )
    plane_place = my_index % plane
    line_place = my_index // plane
    queries = queries.reshape(plane * block_rows, embed)
    passages = passages.reshape(rows_of_planes * block_rows, embed)
    row_pos = all_pos.reshape(plane, 1024)[:, :block_rows].reshape(-1)
    columns = jnp.arange(rows_of_planes * block_rows, dtype=jnp.int32)
    columns = (
        columns // block_rows * plane + plane_place
    ) * block_rows + columns % block_rows

    scores = (
        lax.dot_general(queries, passages, (((1,), (1,)), ((), ())), preferred_element_type=F32)
        * score_scale
    )
    is_positive = row_pos[:, None] == columns[None, :]
    top = jnp.max(scores, axis=1)
    mass = jnp.sum(jnp.exp(scores - top[:, None]), axis=1)
    found = jnp.sum(jnp.where(is_positive, scores, 0.0), axis=1)
    stats = jnp.concatenate([part.reshape(plane, block_rows) for part in (top, mass, found)], axis=1)
    (all_stats,) = exchange(2, device_count, plane, ("plane", "gather", stats))
    tops, masses, founds = (
        all_stats[:, :, part * block_rows : (part + 1) * block_rows] for part in range(3)
    )
    row_top = jnp.max(tops, axis=0)
    log_norm = row_top + jnp.log(jnp.sum(masses * jnp.exp(tops - row_top[None]), axis=0))
    loss_part = jnp.sum(log_norm - jnp.sum(founds, axis=0))
    log_norm = log_norm.reshape(-1)
    weights = (jnp.exp(scores - log_norm[:, None]) - is_positive.astype(F32)).astype(BF16)
    query_part = score_scale * jnp.dot(weights, passages, preferred_element_type=F32)
    passage_part = score_scale * lax.dot_general(
        weights, queries, (((0,), (0,)), ((), ())), preferred_element_type=F32
    )
    query_part = query_part.reshape(plane, block_rows, embed)
    passage_part = passage_part.reshape(rows_of_planes, block_rows, embed)
    query_in, passage_in, losses = exchange(
        3,
        device_count,
        plane,
        ("plane", "scatter", query_part.astype(BF16)),
        ("line", "scatter", passage_part.astype(BF16)),
        ("line", "gather", jnp.broadcast_to(loss_part, (8, 128))),
    )
    mean_loss = jnp.sum(losses[:, 0, 0]) / pair_count
    grads = jnp.concatenate(
        [
            sum_with_own(query_part, query_in, plane_place),
            sum_with_own(passage_part, passage_in, line_place),
        ],
        axis=0,
    ).astype(BF16)
    (pair_grads,) = exchange(4, device_count, plane, ("pair", "gather", grads))

    core = my_index % 2
    half_width = hidden_width // 2
    first_half = lax.dynamic_slice_in_dim(w_first, core * half_width, half_width, 1)
    second_half = lax.dynamic_slice_in_dim(w_second, core * half_width, half_width, 0)
    both = pair_features.reshape(-1, width)
    both_grads = pair_grads.reshape(-1, embed)
    act = jnp.dot(both, first_half, preferred_element_type=F32)
    hid = gelu_tanh(act).astype(BF16)
    back = lax.dot_general(
        both_grads, second_half, (((1,), (1,)), ((), ())), preferred_element_type=F32
    )
    act_grad = jax.vjp(gelu_tanh, act)[1](back)[0].astype(BF16)
    grad_first = lax.dot_general(act_grad, both, (((0,), (0,)), ((), ())), preferred_element_type=F32)
    grad_second = lax.dot_general(hid, both_grads, (((0,), (0,)), ((), ())), preferred_element_type=F32)

    half = rows_of_planes // 2
    lanes_in_plane = plane // 2
    chunk = hidden_width // device_count
    own_first = grad_first.reshape(half, lanes_in_plane, 2 * chunk, width)
    own_second = grad_second.reshape(half, lanes_in_plane, 2 * chunk, embed)
    first_in, second_in = exchange(
        5,
        device_count,
        plane,
        ("lane", "column", own_first.astype(BF16)),
        ("lane", "column", own_second.astype(BF16)),
    )
    lane_place = plane_place // 2
    sum_first = sum_with_own(
        jnp.swapaxes(own_first, 0, 1), first_in, lane_place
    ).reshape(half, 2, chunk, width)
    sum_second = sum_with_own(
        jnp.swapaxes(own_second, 0, 1), second_in, lane_place
    ).reshape(half, 2, chunk, embed)
    chunks = jnp.concatenate([sum_first, sum_second], axis=3)
    landed = last_exchange(6, device_count, plane, chunks.astype(BF16))
    own_chunk = chunks[line_place % half, core]
    slots = jnp.arange(rows_of_planes, dtype=jnp.int32)
    mine = (slots == line_place) & (line_place // half == core)
    total = jnp.sum(jnp.where(mine[:, None, None], own_chunk[None], landed.astype(F32)), axis=0)
    return (mean_loss, total[:, :width].T, total[:, width:])


def solution(mesh):
    return jax.shard_map(
        body,
        mesh=mesh,
        in_specs=(P("dp", None), P("dp", None), P(), P("dp"), P(), P()),
        out_specs=(P(), P(None, "dp"), P("dp", None)),
        check_vma=False,
    )
```

time: 408 us -> 154 us (0.38)
  waiting for transfers between devices: 205 us -> 0 us
  Pallas kernels: 0 us -> 90.5 us
  blocking collectives: 85.3 us -> 0 us
  local copies, waits for them, and re-layouts: 42.6 us -> 8.56 us
  other arithmetic: 12.7 us -> 25.4 us
  matrix products: 34.8 us -> 22.7 us
  between operations: 17.2 us -> 5.5 us
  starting transfers between devices: 5.57 us -> 0 us
    reduce_scatter x2 -> x0, waiting for transfers between devices: 196 us -> none  [the longest x1 113 us: body(): lax.psum_scatter(first_query + first_passage, 'dp', scatter_dimension=1,...]
    pallas_call x0 -> x7, Pallas kernels: none -> 90.5 us  [the longest x6 76.1 us: exchange(): pl.pallas_call(functools.partial(exchange_kernel, size, plane, plan), out...]
    unnamed x1 -> x0, blocking collectives: 45.3 us -> none
    all_gather x1 -> x0, blocking collectives: 40.1 us -> none  [body(): all_pos = lax.all_gather(positives, 'dp', axis=0, tiled=True)]
    gather x5 -> x0, local copies, waits for them, and re-layouts: 33.8 us -> none  [the longest x1 32.5 us: body(): anchor = jnp.take(all_pos, slot_grid)]
    dot_general x11 -> x8, matrix products: 34.8 us -> 22.7 us  [the longest x1 3.99 us: body(): lax.dot_general(act_grad, both, (((0,), (0,)), ((), ())), preferred_eleme...]
    reduce_sum x5 -> x13, other arithmetic: 3.47 us -> 14.8 us  [the longest x4 5.82 us: sum_with_own(): return jnp.sum(jnp.where(mine, own, arrived.astype(F32)), axis=0)]
    ppermute x4 -> x0, waiting for transfers between devices: 8.89 us -> none  [from_partner(): return lax.ppermute(block, axis, route)]
  transfers between devices with their start and end apart: 8 -> 0, of which waited for: 5 -> 0; matrix products, arithmetic and copies ran while one was open for 16% -> 0% of each run, Pallas kernels for 0% -> 0%
where the time goes in v1:
time: 154 us; the launch traced here: 153 us
  Pallas kernels  90.5 us (59%)
  other arithmetic  25.4 us (16%)
  matrix products  22.7 us (15%)
  local copies, waits for them, and re-layouts  8.56 us (6%)
  between operations  5.5 us (4%)
    pallas_call x6, Pallas kernels, exchange(): pl.pallas_call(functools.partial(exchange_kernel, size, plane, plan), out...  76.1 us
    pallas_call x1, Pallas kernels, last_exchange(): pl.pallas_call(functools.partial(last_kernel, size, plane), out_shape=jax...  14.4 us
    reduce_sum x4, other arithmetic, sum_with_own(): return jnp.sum(jnp.where(mine, own, arrived.astype(F32)), axis=0)  5.82 us
    dot_general x1, matrix products, body(): lax.dot_general(act_grad, both, (((0,), (0,)), ((), ())), preferred_eleme...  3.99 us
    dot_general x1, matrix products, body(): lax.dot_general(queries, passages, (((1,), (1,)), ((), ())), preferred_el...  3.61 us
    dot_general x1, matrix products, body(): act = jnp.dot(both, first_half, preferred_element_type=F32)  3.22 us

profile of v1, /device:TPU:9, one launch (start us, length us, event | category | flops | bytes accessed | tf_op | source)
XLA Modules:
  0.0 152.6 jit_solution(18388789937356334265)
XLA Ops:
  0.7 0.9 select_reduce_fusion.7
  1.6 1.3 fusion.52
  2.9 0.2 select_reduce_fusion.6
  3.1 0.8 select_reduce_fusion.5
  3.9 0.7 and_select_fusion.1
  4.7 1.8 %fusion.31.refs_0_ = bf16[15,8,1664]{2,1,0:T(8,128)(2,1)} fusion(bf16[256,128]{1,0:T(8,128)(2,1)S(1)} %select_convert_fusion, bf16[256,768]{1,0:T(8,128)(2,1)} %param.7, bf16[256,768]{1,0:T(8,128)(2,1)} %param.6), kind=kLoop, calls=%fused_computation.49 | loop fusion | flops 1198080 | bytes 1251328 | tf_op jit(solution)/shard_map/reshape | solution.py:243
  6.5 13.7 %shard_map.85 = bf16[16,8,1664]{2,1,0:T(8,128)(2,1)} custom-call(bf16[15,8,1664]{2,1,0:T(8,128)(2,1)} %fusion.31.refs_0_), custom_call_target="tpu_custom_call" | custom-call | tf_op jit(solution)/shard_map/pallas_call | solution.py:104
  20.2 0.6 fusion.53
  23.5 0.8 maximum_select_fusion
  24.3 0.8 pad_maximum_fusion.1.refs_3_
  25.0 2.6 %convolution_convert_fusion = bf16[272,384]{1,0:T(8,128)(2,1)S(1)} fusion(bf16[1536,384]{1,0:T(8,128)(2,1)} %param.11, bf16[768,1536]{1,0:T(8,128)(2,1)S(1)} %copy-done, bf16[8,768]{1,0:T(8,128)(2,1)S(1)} %get-tuple-element.35, bf16[128,768]{1,0:T(8,128)(2,1)S(1)} %slice.58, bf16[8,768]{1,0:T(8,128)(2,1)S(1)} %get-tuple-element.34, ...), kind=kOutput, calls=%fused_computation.31 | convolution fusion | flops 968128512 | bytes 4165632 | tf_op jit(solution)/shard_map/dot_general | solution.py:263
  27.7 0.7 fusion.61
  28.3 0.2 add_reduce_fusion
  28.6 0.6 pad_bitcast_fusion.refs_1_
  29.1 16.6 %shard_map.86 = (bf16[8,136,384]{2,1,0:T(8,128)(2,1)}, s32[8,8,128]{2,1,0:T(8,128)}, bf16[4,136,384]{2,1,0:T(8,128)(2,1)}, bf16[2,272,768]{2,1,0:T(8,128)(2,1)}) custom-call(bf16[136,384]{1,0:T(8,128)(2,1)} %get-tuple-element.33.refs_0_, s32[8,128]{1,0:T(8,128)} %pad_bitcast_fusion.refs_1_, bf16[136,384]{1,0:T(8,128)(2,1)} %get-tuple-element.32.refs_2_, ...), custom_call_target="tpu_custom_call" | custom-call | tf_op jit(solution)/shard_map/pallas_call | solution.py:104
  45.8 3.6 %fusion.63 = (f32[1088]{0:T(1024)S(1)}, f32[1088,544]{0,1:T(8,128)}) fusion(bf16[1088,384]{1,0:T(8,128)(2,1)} %bitcast.64, bf16[544,384]{1,0:T(8,128)(2,1)} %bitcast.68), kind=kOutput, calls=%fused_computation.135 | convolution fusion | flops 455740352 | bytes 3625216 | tf_op jit(solution)/shard_map/dot_general | solution.py:285
  49.6 2.3 %exponential_reduce_fusion = (f32[1088]{0:T(1024)S(1)}, f32[1088]{0:T(1024)S(1)}) fusion(f32[1088,544]{0,1:T(8,128)} %get-tuple-element.40, f32[1088]{0:T(1024)S(1)} %get-tuple-element.39, s32[544]{0:T(1024)S(1)} %fusion.43, s32[1088]{0:T(1024)S(1)} %eq.111), kind=kLoop, calls=%fused_computation.7 | loop fusion | flops 2957184 | bytes 2387072 | tf_op jit(solution)/shard_map/reduce_sum | solution.py:290
  52.1 0.7 pad_maximum_fusion.5.refs_0_
  52.8 5.9 %shard_map.87 = f32[8,8,408]{2,1,0:T(8,128)} custom-call(f32[8,408]{1,0:T(8,128)} %pad_maximum_fusion.5.refs_0_), custom_call_target="tpu_custom_call" | custom-call | tf_op jit(solution)/shard_map/pallas_call | solution.py:104
  58.8 0.9 slice_reduce_fusion.1
  59.6 1.0 slice_reduce_fusion
  60.7 0.6 subtract_reduce_fusion
  61.4 3.0 %convolution_multiply_fusion.2 = f32[544,384]{1,0:T(8,128)S(1)} fusion(bf16[1088,384]{1,0:T(8,128)(2,1)} %bitcast.65, f32[1088,544]{0,1:T(8,128)} %get-tuple-element.40, f32[1088]{0:T(1024)S(1)} %add.179, s32[1088]{0:T(1024)S(1)} %eq.111, s32[544]{0:T(1024)S(1)} %fusion.43), kind=kOutput, calls=%fused_computation.30 | convolution fusion | flops 457725952 | bytes 4049536 | tf_op jit(solution)/shard_map/dot_general | solution.py:303
  64.3 0.8 convert_element_type.78.refs_1_
  65.2 1.1 convolution_multiply_fusion.1
  66.3 1.2 copy-done.2
  67.5 1.0 convert_element_type.77.refs_0_
  68.5 1.2 broadcast_in_dim.172.refs_2_
  69.8 14.5 %shard_map.88 = (bf16[8,136,384]{2,1,0:T(8,128)(2,1)}, bf16[4,136,384]{2,1,0:T(8,128)(2,1)}, f32[4,8,128]{2,1,0:T(8,128)}) custom-call(bf16[8,136,384]{2,1,0:T(8,128)(2,1)} %convert_element_type.77.refs_0_, bf16[4,136,384]{2,1,0:T(8,128)(2,1)} %convert_element_type.78.refs_1_, f32[8,128]{1,0:T(8,128)} %broadcast_in_dim.172.refs_2_), custom_call_target="tpu_custom_call" | custom-call | tf_op jit(solution)/shard_map/pallas_call | solution.py:104
  84.3 1.9 %select_reduce_fusion = bf16[136,384]{1,0:T(8,128)(2,1)S(1)} fusion(f32[8,136,384]{2,1,0:T(8,128)} %bitcast.53, bf16[8,136,384]{2,1,0:T(8,128)(2,1)} %get-tuple-element.16, pred[8]{0:T(512)(128)(4,1)S(1)} %iota_compare_fusion.1), kind=kLoop, calls=%fused_computation.29 | loop fusion | flops 1201152 | bytes 2611208 | tf_op jit(solution)/shard_map/reduce_sum | solution.py:195
  86.2 1.2 select_reduce_fusion.2
  87.4 0.7 pad_maximum_fusion.4.refs_0_
  88.1 2.5 %shard_map.89 = bf16[2,272,384]{2,1,0:T(8,128)(2,1)} custom-call(bf16[272,384]{1,0:T(8,128)(2,1)} %pad_maximum_fusion.4.refs_0_), custom_call_target="tpu_custom_call" | custom-call | tf_op jit(solution)/shard_map/pallas_call | solution.py:104
  90.7 3.2 %multiply_convert_fusion = (bf16[768,544]{0,1:T(8,128)(2,1)}, f32[768,544]{0,1:T(8,128)S(1)}) fusion(bf16[544,768]{1,0:T(8,128)(2,1)} %bitcast.66, bf16[768,1536]{1,0:T(8,128)(2,1)S(1)} %copy-done, s32[]{:T(128)S(6)} %select_n.200), kind=kOutput, calls=%fused_computation.28 | convolution fusion | flops 645488640 | bytes 4521988 | tf_op jit(solution)/shard_map/dot_general | solution.py:332
  93.9 2.2 %fusion.10 = bf16[768,544]{0,1:T(8,128)(2,1)} fusion(f32[768,544]{0,1:T(8,128)S(1)} %get-tuple-element.42, bf16[544,384]{1,0:T(8,128)(2,1)S(1)} %bitcast.63, bf16[1536,384]{1,0:T(8,128)(2,1)S(1)} %copy-done.10, s32[]{:T(128)S(6)} %select_n.200), kind=kOutput, calls=%fused_computation.19 | convolution fusion | flops 329220096 | bytes 3514372 | tf_op jit(solution)/shard_map/dot_general | solution.py:334
  96.1 1.5 copy.17
  97.7 4.0 %fusion.64 = (bf16[2,4,96,768]{3,2,1,0:T(8,128)(2,1)}, f32[2,4,96,768]{3,2,1,0:T(8,128)}) fusion(bf16[2,4,96,544]{3,2,1,0:T(8,128)(2,1)S(1)} %bitcast.56, bf16[544,768,1,1]{1,0,3,2:T(8,128)(2,1)} %bitcast.67), kind=kOutput, calls=%fused_computation.136 | convolution fusion | flops 642318336 | bytes 5210112 | tf_op jit(solution)/shard_map/dot_general | solution.py:338
  101.7 1.5 copy.19
  103.2 2.9 %fusion.65 = (bf16[2,4,96,384]{3,2,1,0:T(8,128)(2,1)}, f32[2,4,96,384]{3,2,1,0:T(8,128)}) fusion(bf16[2,4,96,544]{3,2,1,0:T(8,128)(2,1)S(1)} %bitcast.57, bf16[544,384,1,1]{1,0,3,2:T(8,128)(2,1)} %bitcast.62), kind=kOutput, calls=%fused_computation.137 | convolution fusion | flops 321159168 | bytes 3022848 | tf_op jit(solution)/shard_map/dot_general | solution.py:339
  106.1 22.8 %shard_map.90 = (bf16[4,2,96,768]{3,2,1,0:T(8,128)(2,1)}, bf16[4,2,96,384]{3,2,1,0:T(8,128)(2,1)}) custom-call(bf16[2,4,96,768]{3,2,1,0:T(8,128)(2,1)} %get-tuple-element.43.refs_0_, bf16[2,4,96,384]{3,2,1,0:T(8,128)(2,1)} %get-tuple-element.45.refs_1_), custom_call_target="tpu_custom_call" | custom-call | tf_op jit(solution)/shard_map/pallas_call | solution.py:104
  129.0 2.5 %fusion.3 = f32[2,96,768]{2,1,0:T(8,128)S(1)} fusion(f32[2,4,96,768]{3,2,1,0:T(8,128)} %get-tuple-element.44, bf16[4,2,96,768]{3,2,1,0:T(8,128)(2,1)} %get-tuple-element.19, pred[4]{0:T(512)(128)(4,1)S(1)} %iota_compare_fusion.2), kind=kLoop, calls=%fused_computation.12 | loop fusion | flops 1622016 | bytes 4128772 | tf_op jit(solution)/shard_map/reduce_sum | solution.py:195
  131.6 0.2 fusion.19
  131.8 0.8 fusion.22.source
  132.7 14.4 %shard_map.91 = bf16[4,48,1152]{2,1,0:T(8,128)(2,1)} custom-call(bf16[2,2,48,1152]{3,2,1,0:T(8,128)(2,1)} %fusion.22.source), custom_call_target="tpu_custom_call" | custom-call | tf_op jit(solution)/shard_map/pallas_call | solution.py:179
  147.0 1.2 select_reduce_fusion.1
  148.2 0.7 slice_bitcast_fusion
  148.9 0.6 slice.80
  149.5 1.3 slice_reduce_fusion.2
  (41 shorter events, 0.7 us)
Async XLA Ops:
  0.6 24.4 %copy-start = (bf16[768,1536]{1,0:T(8,128)(2,1)S(1)}, bf16[768,1536]{1,0:T(8,128)(2,1)}, u32[]{:S(2)}) copy-start(bf16[768,1536]{1,0:T(8,128)(2,1)} %param.10) | copy-start | bytes 7077892
  0.6 22.8 %copy-start.4 = (bf16[256,768]{1,0:T(8,128)(2,1)S(1)}, bf16[256,768]{1,0:T(8,128)(2,1)}, u32[]{:S(2)}) copy-start(bf16[256,768]{1,0:T(8,128)(2,1)} %param.6) | copy-start | bytes 1179652
  0.7 22.8 %copy-start.5 = (bf16[256,768]{1,0:T(8,128)(2,1)S(1)}, bf16[256,768]{1,0:T(8,128)(2,1)}, u32[]{:S(2)}) copy-start(bf16[256,768]{1,0:T(8,128)(2,1)} %param.7) | copy-start | bytes 1179652
  45.8 3.6 %copy-start.9 = (s32[8,8,128]{2,1,0:T(8,128)S(1)}, s32[8,8,128]{2,1,0:T(8,128)}, u32[]{:S(2)}) copy-start(s32[8,8,128]{2,1,0:T(8,128)} %get-tuple-element.14) | copy-start | bytes 98308
  61.4 3.8 %copy-start.1 = (f32[1088,544]{0,1:T(8,128)S(1)}, f32[1088,544]{0,1:T(8,128)}, u32[]{:S(2)}) copy-start(f32[1088,544]{0,1:T(8,128)} %get-tuple-element.40) | copy-start | bytes 7102468
  61.4 3.8 %copy-start.8 = (bf16[4,136,384]{2,1,0:T(8,128)(2,1)S(1)}, bf16[4,136,384]{2,1,0:T(8,128)(2,1)}, u32[]{:S(2)}) copy-start(bf16[4,136,384]{2,1,0:T(8,128)(2,1)} %get-tuple-element.13) | copy-start | bytes 1253380
  66.3 1.2 copy-start.2
  90.7 3.2 %copy-start.6 = (bf16[2,272,384]{2,1,0:T(8,128)(2,1)S(1)}, bf16[2,272,384]{2,1,0:T(8,128)(2,1)}, u32[]{:S(2)}) copy-start(bf16[2,272,384]{2,1,0:T(8,128)(2,1)} %shard_map.89) | copy-start | bytes 1253380
  90.7 3.2 %copy-start.10 = (bf16[1536,384]{1,0:T(8,128)(2,1)S(1)}, bf16[1536,384]{1,0:T(8,128)(2,1)}, u32[]{:S(2)}) copy-start(bf16[1536,384]{1,0:T(8,128)(2,1)} %param.11) | copy-start | bytes 3538948
  129.0 2.5 %copy-start.3 = (f32[2,4,96,384]{3,2,1,0:T(8,128)S(1)}, f32[2,4,96,384]{3,2,1,0:T(8,128)}, u32[]{:S(2)}) copy-start(f32[2,4,96,384]{3,2,1,0:T(8,128)} %get-tuple-element.46) | copy-start | bytes 3538948
  129.0 2.5 %copy-start.7 = (bf16[4,2,96,384]{3,2,1,0:T(8,128)(2,1)S(1)}, bf16[4,2,96,384]{3,2,1,0:T(8,128)(2,1)}, u32[]{:S(2)}) copy-start(bf16[4,2,96,384]{3,2,1,0:T(8,128)(2,1)} %get-tuple-element.20) | copy-start | bytes 1769476

commit v2 on v1

--- a/solution.py
+++ b/solution.py
@@ -117,47 +117,156 @@
     )(*arrays)
 
 
-def last_kernel(size, plane, source, landing, send_sem, recv_sem):
+GELU_ROOT = 0.7978845608028654
+GELU_CUBE = 0.044715
+
+
+def gelu_and_slope(value):
+    square = value * value
+    bent = jnp.tanh(GELU_ROOT * value * (1.0 + GELU_CUBE * square))
+    rise = 0.5 * (1.0 + bent)
+    slope = rise + 0.5 * value * (1.0 - bent * bent) * (
+        GELU_ROOT * (1.0 + 3.0 * GELU_CUBE * square)
+    )
+    return value * rise, slope
+
+
+def dot(left, right, left_dim, right_dim):
+    return lax.dot_general(
+        left, right, (((left_dim,), (right_dim,)), ((), ())), preferred_element_type=F32
+    )
+
+
+TILES = 2
+
+
+def tail_kernel(
+    size,
+    plane,
+    features,
+    grads,
+    w_first,
+    w_second,
+    out_first,
+    out_second,
+    both_grads,
+    own,
+    outgoing,
+    landing,
+    sums,
+    forward,
+    landed,
+    pair_sems,
+    lane_send,
+    lane_recv,
+    line_send,
+    line_recv,
+):
     me = lax.axis_index("dp")
     rows = size // plane
     half = rows // 2
+    lanes = plane // 2
     row = lax.div(me, plane)
     core = lax.rem(me, 2)
+    lane = lax.div(lax.rem(me, plane), 2)
     column = lax.rem(me, plane) - core
+    width = features.shape[1]
+    local_rows = grads.shape[0]
+    hidden_half = w_second.shape[0] // 2
+    tile = hidden_half // TILES
+    per_tile = half // TILES
+    chunk = hidden_half // (half * lanes * 2)
+
     barrier = pltpu.get_barrier_semaphore()
     spot = 2 * row + core
     for k in range(1, 2 * rows):
         other = lax.rem(spot + k, 2 * rows)
         index = plane * lax.div(other, 2) + column + lax.rem(other, 2)
         pl.semaphore_signal(barrier, inc=1, device_id=(index,), device_id_type=MESH)
-    pl.semaphore_wait(barrier, 2 * rows - 1)
+    for k in range(1, lanes):
+        index = plane * row + 2 * lax.rem(lane + k, lanes) + core
+        pl.semaphore_signal(barrier, inc=1, device_id=(index,), device_id_type=MESH)
+    pl.semaphore_wait(barrier, 2 * rows + lanes - 2)
+
+    pair_copy = pltpu.make_async_remote_copy(
+        src_ref=grads,
+        dst_ref=both_grads.at[core],
+        send_sem=pair_sems.at[0],
+        recv_sem=pair_sems.at[1],
+        device_id=(me + 1 - 2 * core,),
+        device_id_type=MESH,
+    )
+    pair_copy.start()
+    both_grads[core] = grads[...]
+
+    def lane_copy(t, k):
+        there = lax.rem(lane + k, lanes)
+        return pltpu.make_async_remote_copy(
+            src_ref=outgoing.at[pl.ds(t * per_tile, per_tile), there],
+            dst_ref=landing.at[lane, pl.ds(t * per_tile, per_tile)],
+            send_sem=lane_send.at[t, k],
+            recv_sem=lane_recv.at[t, k],
+            device_id=(plane * row + 2 * there + core,),
+            device_id_type=MESH,
+        )
+
+    for t in range(TILES):
+        start = pl.multiple_of(core * hidden_half + t * tile, 128)
+        act = dot(features[...], w_first[:, pl.ds(start, tile)], 1, 0)
+        hidden, slope = gelu_and_slope(act)
+        hidden = hidden.astype(BF16)
+        if t == 0:
+            pair_copy.wait()
+        de = both_grads[...].reshape(2 * local_rows, -1)
+        back = dot(de, w_second[pl.ds(start, tile), :], 1, 1)
+        act_grad = (slope * back).astype(BF16)
+        first = dot(act_grad, features[...], 0, 0)
+        second = dot(hidden, de, 0, 0)
+        for i in range(per_tile):
+            for m in range(lanes):
+                for j in range(2):
+                    at = ((i * lanes + m) * 2 + j) * chunk
+                    for part, low in ((first, 0), (second, width)):
+                        high = low + part.shape[1]
+                        piece = part[at : at + chunk]
+                        own[t * per_tile + i, m, j, :, low:high] = piece
+                        outgoing[t * per_tile + i, m, j, :, low:high] = piece.astype(BF16)
+        for k in range(1, lanes):
+            lane_copy(t, k).start()
+
     sender_core = lax.div(row, half)
 
-    def copy_of(i, j):
+    def line_copy(i, j):
         return pltpu.make_async_remote_copy(
-            src_ref=source.at[i, j],
-            dst_ref=landing.at[row],
-            send_sem=send_sem.at[i, j],
-            recv_sem=recv_sem.at[row],
+            src_ref=forward.at[i, j],
+            dst_ref=landed.at[row],
+            send_sem=line_send.at[i, j],
+            recv_sem=line_recv.at[row],
             device_id=(plane * (half * core + i) + column + j,),
             device_id_type=MESH,
         )
 
+    for t in range(TILES):
+        for k in range(1, lanes):
+            lane_copy(t, k).wait()
+        for i in range(t * per_tile, (t + 1) * per_tile):
+            for j in range(2):
+                total = own[i, lane, j]
+                for k in range(1, lanes):
+                    total = total + landing[lax.rem(lane + k, lanes), i, j].astype(F32)
+                sums[i, j] = total
+                forward[i, j] = total.astype(BF16)
+
+                @pl.when(plane * (half * core + i) + column + j != me)
+                def _():
+                    line_copy(i, j).start()
+
     for i in range(half):
         for j in range(2):
-            target = plane * (half * core + i) + column + j
-
-            @pl.when(target != me)
+
+            @pl.when(plane * (half * core + i) + column + j != me)
             def _():
-                copy_of(i, j).start()
-
-    for i in range(half):
-        for j in range(2):
-            target = plane * (half * core + i) + column + j
-
-            @pl.when(target != me)
-            def _():
-                copy_of(i, j).wait_send()
+                line_copy(i, j).wait_send()
 
     for sender_row in range(rows):
         sender = plane * sender_row + column + sender_core
@@ -165,28 +274,56 @@
         @pl.when(sender != me)
         def _():
             pltpu.make_async_remote_copy(
-                src_ref=source.at[0, 0],
-                dst_ref=landing.at[sender_row],
-                send_sem=send_sem.at[0, 0],
-                recv_sem=recv_sem.at[sender_row],
+                src_ref=forward.at[0, 0],
+                dst_ref=landed.at[sender_row],
+                send_sem=line_send.at[0, 0],
+                recv_sem=line_recv.at[sender_row],
                 device_id=(sender,),
                 device_id_type=MESH,
             ).wait_recv()
 
-
-def last_exchange(name, size, plane, chunks):
-    rows = size // plane
+    total = jnp.where(sender_core == core, sums[lax.rem(row, half), core], 0.0)
+    for sender_row in range(rows):
+        sender = plane * sender_row + column + sender_core
+        total = total + jnp.where(sender == me, 0.0, landed[sender_row].astype(F32))
+    out_first[...] = total[:, :width]
+    out_second[...] = total[:, width:]
+
+
+def finish(name, size, plane, features, grads, w_first, w_second):
+    rows, lanes = size // plane, plane // 2
+    half = rows // 2
+    width, hidden_width = w_first.shape
+    embed = w_second.shape[1]
+    chunk = hidden_width // size
+    across = width + embed
+    vmem = pl.BlockSpec(memory_space=pltpu.VMEM)
     return pl.pallas_call(
-        functools.partial(last_kernel, size, plane),
-        out_shape=jax.ShapeDtypeStruct((rows,) + chunks.shape[2:], chunks.dtype),
-        in_specs=[pl.BlockSpec(memory_space=pl.ANY)],
-        out_specs=pl.BlockSpec(memory_space=pl.ANY),
+        functools.partial(tail_kernel, size, plane),
+        out_shape=[
+            jax.ShapeDtypeStruct((chunk, width), F32),
+            jax.ShapeDtypeStruct((chunk, embed), F32),
+        ],
+        in_specs=[vmem] * 4,
+        out_specs=[vmem] * 2,
         scratch_shapes=[
-            pltpu.SemaphoreType.DMA((rows // 2, 2)),
+            pltpu.VMEM((2,) + grads.shape, BF16),
+            pltpu.VMEM((half, lanes, 2, chunk, across), F32),
+            pltpu.VMEM((half, lanes, 2, chunk, across), BF16),
+            pltpu.VMEM((lanes, half, 2, chunk, across), BF16),
+            pltpu.VMEM((half, 2, chunk, across), F32),
+            pltpu.VMEM((half, 2, chunk, across), BF16),
+            pltpu.VMEM((rows, chunk, across), BF16),
+            pltpu.SemaphoreType.DMA((2,)),
+            pltpu.SemaphoreType.DMA((TILES, lanes)),
+            pltpu.SemaphoreType.DMA((TILES, lanes)),
+            pltpu.SemaphoreType.DMA((half, 2)),
             pltpu.SemaphoreType.DMA((rows,)),
         ],
-        compiler_params=pltpu.CompilerParams(collective_id=name, has_side_effects=True),
-    )(chunks)
+        compiler_params=pltpu.CompilerParams(
+            collective_id=name, has_side_effects=True, vmem_limit_bytes=50 * 1024 * 1024
+        ),
+    )(features, grads, w_first, w_second)
 
 
 def sum_with_own(own, arrived, place):
@@ -321,49 +458,10 @@
         ],
         axis=0,
     ).astype(BF16)
-    (pair_grads,) = exchange(4, device_count, plane, ("pair", "gather", grads))
-
-    core = my_index % 2
-    half_width = hidden_width // 2
-    first_half = lax.dynamic_slice_in_dim(w_first, core * half_width, half_width, 1)
-    second_half = lax.dynamic_slice_in_dim(w_second, core * half_width, half_width, 0)
-    both = pair_features.reshape(-1, width)
-    both_grads = pair_grads.reshape(-1, embed)
-    act = jnp.dot(both, first_half, preferred_element_type=F32)
-    hid = gelu_tanh(act).astype(BF16)
-    back = lax.dot_general(
-        both_grads, second_half, (((1,), (1,)), ((), ())), preferred_element_type=F32
-    )
-    act_grad = jax.vjp(gelu_tanh, act)[1](back)[0].astype(BF16)
-    grad_first = lax.dot_general(act_grad, both, (((0,), (0,)), ((), ())), preferred_element_type=F32)
-    grad_second = lax.dot_general(hid, both_grads, (((0,), (0,)), ((), ())), preferred_element_type=F32)
-
-    half = rows_of_planes // 2
-    lanes_in_plane = plane // 2
-    chunk = hidden_width // device_count
-    own_first = grad_first.reshape(half, lanes_in_plane, 2 * chunk, width)
-    own_second = grad_second.reshape(half, lanes_in_plane, 2 * chunk, embed)
-    first_in, second_in = exchange(
-        5,
-        device_count,
-        plane,
-        ("lane", "column", own_first.astype(BF16)),
-        ("lane", "column", own_second.astype(BF16)),
-    )
-    lane_place = plane_place // 2
-    sum_first = sum_with_own(
-        jnp.swapaxes(own_first, 0, 1), first_in, lane_place
-    ).reshape(half, 2, chunk, width)
-    sum_second = sum_with_own(
-        jnp.swapaxes(own_second, 0, 1), second_in, lane_place
-    ).reshape(half, 2, chunk, embed)
-    chunks = jnp.concatenate([sum_first, sum_second], axis=3)
-    landed = last_exchange(6, device_count, plane, chunks.astype(BF16))
-    own_chunk = chunks[line_place % half, core]
-    slots = jnp.arange(rows_of_planes, dtype=jnp.int32)
-    mine = (slots == line_place) & (line_place // half == core)
-    total = jnp.sum(jnp.where(mine[:, None, None], own_chunk[None], landed.astype(F32)), axis=0)
-    return (mean_loss, total[:, :width].T, total[:, width:])
+    total_first, total_second = finish(
+        4, device_count, plane, pair_features.reshape(-1, width), grads, w_first, w_second
+    )
+    return (mean_loss, total_first.T, total_second)
 
 
 def solution(mesh):

time: 154 us -> 130 us (0.84)
  matrix products: 22.7 us -> 10.5 us
  other arithmetic: 25.4 us -> 20 us
  Pallas kernels: 90.5 us -> 85.7 us
  local copies, waits for them, and re-layouts: 8.56 us -> 6.94 us
    pallas_call x6 -> x4, Pallas kernels: 76.1 us -> 50.8 us  [exchange(): pl.pallas_call(functools.partial(exchange_kernel, size, plane, plan), out...]
    pallas_call x1, Pallas kernels: 14.4 us -> 34.9 us  [finish(): pl.pallas_call(functools.partial(tail_kernel, size, plane), out_shape=[ja...]
    dot_general x4 -> x0, matrix products: 12.4 us -> none  [the longest x1 3.99 us: body(): lax.dot_general(act_grad, both, (((0,), (0,)), ((), ())), preferred_eleme...]
    convert_element_type x2 -> x0, local copies, waits for them, and re-layouts: 3.05 us -> none  [the longest x1 1.52 us: body(): act_grad = jax.vjp(gelu_tanh, act)[1](back)[0].astype(BF16)]
    reduce_sum x4 -> x2, other arithmetic: 5.82 us -> 3.14 us  [sum_with_own(): return jnp.sum(jnp.where(mine, own, arrived.astype(F32)), axis=0)]
where the time goes in v2:
time: 130 us; the launch traced here: 128 us
  Pallas kernels  85.7 us (66%)
  other arithmetic  20 us (15%)
  matrix products  10.5 us (8%)
  local copies, waits for them, and re-layouts  6.94 us (5%)
  between operations  5.33 us (4%)
    pallas_call x4, Pallas kernels, exchange(): pl.pallas_call(functools.partial(exchange_kernel, size, plane, plan), out...  50.8 us
    pallas_call x1, Pallas kernels, finish(): pl.pallas_call(functools.partial(tail_kernel, size, plane), out_shape=[ja...  34.9 us
    dot_general x1, matrix products, body(): lax.dot_general(queries, passages, (((1,), (1,)), ((), ())), preferred_el...  3.58 us
    reduce_sum x2, other arithmetic, sum_with_own(): return jnp.sum(jnp.where(mine, own, arrived.astype(F32)), axis=0)  3.14 us
    dot_general x1, matrix products, body(): jnp.dot(hidden, w_second, preferred_element_type=F32).astype(BF16)  3 us
    dot_general x1, matrix products, body(): lax.dot_general(weights, queries, (((0,), (0,)), ((), ())), preferred_ele...  2.76 us

profile of v2, /device:TPU:9, one launch (start us, length us, event | category | flops | bytes accessed | tf_op | source)
XLA Modules:
  0.0 128.5 jit_solution(9721484537945195890)
XLA Ops:
  0.6 0.0 copy-start.4
  0.6 0.0 copy-start.5
  0.7 0.0 copy-start
  0.7 0.9 select_reduce_fusion.6
  1.6 1.3 %fusion.32 = (s32[]{:T(128)}, s32[32]{0:T(128)S(1)}, s32[32]{0:T(128)S(1)}, s32[32]{0:T(128)S(1)}) fusion(s32[32]{0:T(128)} %param.8, s32[]{:T(128)S(6)} %axis_index.12, s32[32]{0:T(128)S(1)} %select_reduce_fusion.6), kind=kLoop, calls=%fused_computation.89 | loop fusion | flops 607 | bytes 648 | tf_op jit(solution)/shard_map/reduce_sum | solution.py:355
  3.6 0.2 select_reduce_fusion.5
  3.7 0.6 fusion.33
  6.3 0.8 select_reduce_fusion.4
  7.1 0.7 and_select_fusion.1
  7.9 0.1 select_convert_fusion
  8.0 0.9 slice.48
  8.9 0.9 slice.52
  9.9 1.8 %fusion.15.refs_0_ = bf16[15,8,1664]{2,1,0:T(8,128)(2,1)} fusion(bf16[256,128]{1,0:T(8,128)(2,1)S(1)} %select_convert_fusion, bf16[256,768]{1,0:T(8,128)(2,1)} %param.7, bf16[256,768]{1,0:T(8,128)(2,1)} %param.6), kind=kLoop, calls=%fused_computation.26 | loop fusion | flops 1198080 | bytes 1251328 | tf_op jit(solution)/shard_map/reshape | solution.py:380
  11.7 13.7 %shard_map.85 = bf16[16,8,1664]{2,1,0:T(8,128)(2,1)} custom-call(bf16[15,8,1664]{2,1,0:T(8,128)(2,1)} %fusion.15.refs_0_), custom_call_target="tpu_custom_call" | custom-call | tf_op jit(solution)/shard_map/pallas_call | solution.py:104
  25.4 0.0 copy-done.4
  25.4 0.0 copy-done.5
  25.4 0.8 maximum_select_fusion
  26.2 0.2 add_reduce_fusion
  26.4 0.6 pad_bitcast_fusion.refs_1_
  27.0 3.0 %convolution_convert_fusion = bf16[272,384]{1,0:T(8,128)(2,1)S(1)} fusion(bf16[1536,384]{1,0:T(8,128)(2,1)S(1)} %copy-done, bf16[768,1536]{1,0:T(8,128)(2,1)} %w_first.1, bf16[8,768]{1,0:T(8,128)(2,1)S(1)} %get-tuple-element.35, bf16[128,768]{1,0:T(8,128)(2,1)S(1)} %slice.52, bf16[8,768]{1,0:T(8,128)(2,1)S(1)} %get-tuple-element.34, ...), kind=kOutput, calls=%fused_computation.19 | convolution fusion | flops 968128512 | bytes 4165632 | tf_op jit(solution)/shard_map/dot_general | solution.py:400
  30.0 0.8 pad_maximum_fusion.refs_3_
  30.8 0.7 fusion.41
  31.5 16.6 %shard_map.86 = (bf16[8,136,384]{2,1,0:T(8,128)(2,1)}, s32[8,8,128]{2,1,0:T(8,128)}, bf16[4,136,384]{2,1,0:T(8,128)(2,1)}, bf16[2,272,768]{2,1,0:T(8,128)(2,1)}) custom-call(bf16[136,384]{1,0:T(8,128)(2,1)} %get-tuple-element.33.refs_0_, s32[8,128]{1,0:T(8,128)} %pad_bitcast_fusion.refs_1_, bf16[136,384]{1,0:T(8,128)(2,1)} %get-tuple-element.32.refs_2_, ...), custom_call_target="tpu_custom_call" | custom-call | tf_op jit(solution)/shard_map/pallas_call | solution.py:104
  48.1 0.8 copy.11
  48.9 0.1 eq.89
  49.0 3.6 %fusion.43 = (f32[1088]{0:T(1024)S(1)}, f32[1088,544]{0,1:T(8,128)}) fusion(bf16[1088,384]{1,0:T(8,128)(2,1)} %bitcast.28, bf16[544,384]{1,0:T(8,128)(2,1)} %bitcast.30), kind=kOutput, calls=%fused_computation.105 | convolution fusion | flops 455740352 | bytes 3625216 | tf_op jit(solution)/shard_map/dot_general | solution.py:422
  52.6 0.1 reshape.154
  52.7 2.4 %exponential_reduce_fusion = (f32[1088]{0:T(1024)S(1)}, f32[1088]{0:T(1024)S(1)}) fusion(f32[1088,544]{0,1:T(8,128)} %get-tuple-element.40, f32[1088]{0:T(1024)S(1)} %get-tuple-element.39, s32[544]{0:T(1024)S(1)} %fusion.25, s32[1088]{0:T(1024)S(1)} %eq.89), kind=kLoop, calls=%fused_computation.7 | loop fusion | flops 2957184 | bytes 2387072 | tf_op jit(solution)/shard_map/reduce_sum | solution.py:427
  55.0 0.1 reshape.155
  55.1 0.1 reshape.157
  55.2 0.7 pad_maximum_fusion.4.refs_0_
  55.9 5.9 %shard_map.87 = f32[8,8,408]{2,1,0:T(8,128)} custom-call(f32[8,408]{1,0:T(8,128)} %pad_maximum_fusion.4.refs_0_), custom_call_target="tpu_custom_call" | custom-call | tf_op jit(solution)/shard_map/pallas_call | solution.py:104
  61.8 0.9 slice_reduce_fusion.1
  62.7 1.0 slice_reduce_fusion
  63.7 0.6 subtract_reduce_fusion
  64.3 0.1 add.148
  64.4 2.8 %convolution_multiply_fusion.2 = f32[544,384]{1,0:T(8,128)S(1)} fusion(bf16[1088,384]{1,0:T(8,128)(2,1)S(1)} %bitcast.29, f32[1088,544]{0,1:T(8,128)} %get-tuple-element.40, f32[1088]{0:T(1024)S(1)} %add.148, s32[1088]{0:T(1024)S(1)} %eq.89, s32[544]{0:T(1024)S(1)} %fusion.25), kind=kOutput, calls=%fused_computation.18 | convolution fusion | flops 457725952 | bytes 4049536 | tf_op jit(solution)/shard_map/dot_general | solution.py:440
  67.2 1.2 convolution_multiply_fusion.1
  68.4 1.3 broadcast_in_dim.137.refs_2_
  69.7 0.8 convert_element_type.52.refs_1_
  70.5 1.0 convert_element_type.51.refs_0_
  71.5 14.5 %shard_map.88 = (bf16[8,136,384]{2,1,0:T(8,128)(2,1)}, bf16[4,136,384]{2,1,0:T(8,128)(2,1)}, f32[4,8,128]{2,1,0:T(8,128)}) custom-call(bf16[8,136,384]{2,1,0:T(8,128)(2,1)} %convert_element_type.51.refs_0_, bf16[4,136,384]{2,1,0:T(8,128)(2,1)} %convert_element_type.52.refs_1_, f32[8,128]{1,0:T(8,128)} %broadcast_in_dim.137.refs_2_), custom_call_target="tpu_custom_call" | custom-call | tf_op jit(solution)/shard_map/pallas_call | solution.py:104
  86.0 1.2 select_reduce_fusion.1
  87.3 1.9 %select_reduce_fusion = bf16[136,384]{1,0:T(8,128)(2,1)S(1)} fusion(f32[8,136,384]{2,1,0:T(8,128)} %bitcast.25, bf16[8,136,384]{2,1,0:T(8,128)(2,1)} %get-tuple-element.17, pred[8]{0:T(512)(128)(4,1)S(1)} %iota_compare_fusion.2), kind=kLoop, calls=%fused_computation.17 | loop fusion | flops 1201152 | bytes 2611208 | tf_op jit(solution)/shard_map/reduce_sum | solution.py:332
  89.1 1.3 %slice_reduce_fusion.2 = f32[]{:T(128)} fusion(f32[4,8,128]{2,1,0:T(8,128)} %get-tuple-element.15), kind=kLoop, calls=%fused_computation.64 | loop fusion | flops 3 | bytes 20 | tf_op jit(solution)/shard_map/reduce_sum | solution.py:453
  91.2 34.9 %shard_map.89 = (f32[48,768]{1,0:T(8,128)S(1)}, f32[48,384]{1,0:T(8,128)S(1)}) custom-call(bf16[544,768]{1,0:T(8,128)(2,1)S(1)} %bitcast.22, bf16[272,384]{1,0:T(8,128)(2,1)S(1)} %pad_maximum_fusion.3.grads, bf16[768,1536]{1,0:T(8,128)(2,1)} %w_first.1, bf16[1536,384]{1,0:T(8,128)(2,1)S(1)} %copy-done), custom_call_target="tpu_custom_call" | custom-call | tf_op jit(solution)/shard_map/pallas_call | solution.py:301
  126.1 0.7 copy.14
  126.7 0.6 copy.15
  (21 shorter events, 0.1 us)
Async XLA Ops:
  0.6 24.8 %copy-start.4 = (bf16[256,768]{1,0:T(8,128)(2,1)S(1)}, bf16[256,768]{1,0:T(8,128)(2,1)}, u32[]{:S(2)}) copy-start(bf16[256,768]{1,0:T(8,128)(2,1)} %param.7) | copy-start | bytes 1179652
  0.6 24.8 %copy-start.5 = (bf16[256,768]{1,0:T(8,128)(2,1)S(1)}, bf16[256,768]{1,0:T(8,128)(2,1)}, u32[]{:S(2)}) copy-start(bf16[256,768]{1,0:T(8,128)(2,1)} %param.6) | copy-start | bytes 1179652
  0.7 26.3 %copy-start = (bf16[1536,384]{1,0:T(8,128)(2,1)S(1)}, bf16[1536,384]{1,0:T(8,128)(2,1)}, u32[]{:S(2)}) copy-start(bf16[1536,384]{1,0:T(8,128)(2,1)} %w_second.1) | copy-start | bytes 3538948
  52.6 11.9 %copy-start.6 = (bf16[8,136,384]{2,1,0:T(8,128)(2,1)S(1)}, bf16[8,136,384]{2,1,0:T(8,128)(2,1)}, u32[]{:S(2)}) copy-start(bf16[8,136,384]{2,1,0:T(8,128)(2,1)} %get-tuple-element.12) | copy-start | bytes 2506756
  64.4 2.8 %copy-start.2 = (f32[1088,544]{0,1:T(8,128)S(1)}, f32[1088,544]{0,1:T(8,128)}, u32[]{:S(2)}) copy-start(f32[1088,544]{0,1:T(8,128)} %get-tuple-element.40) | copy-start | bytes 7102468
  64.4 2.8 %copy-start.7 = (bf16[4,136,384]{2,1,0:T(8,128)(2,1)S(1)}, bf16[4,136,384]{2,1,0:T(8,128)(2,1)}, u32[]{:S(2)}) copy-start(bf16[4,136,384]{2,1,0:T(8,128)(2,1)} %get-tuple-element.13) | copy-start | bytes 1253380
  68.4 2.1 %copy-start.3 = (f32[1088,384]{1,0:T(8,128)}, f32[1088,384]{1,0:T(8,128)S(1)}, u32[]{:S(2)}) copy-start(f32[1088,384]{1,0:T(8,128)S(1)} %convolution_multiply_fusion.1) | copy-start | bytes 5013508
  86.0 5.2 %copy-start.1 = (bf16[2,272,768]{2,1,0:T(8,128)(2,1)S(1)}, bf16[2,272,768]{2,1,0:T(8,128)(2,1)}, u32[]{:S(2)}) copy-start(bf16[2,272,768]{2,1,0:T(8,128)(2,1)} %get-tuple-element.16) | copy-start | bytes 2506756

commit v3 on v0

v3 whole, which is shorter than its diff:
```python
import functools

import jax
import jax.numpy as jnp
from jax import lax
from jax.experimental import pallas as pl
from jax.experimental.pallas import tpu as pltpu
from jax.sharding import PartitionSpec as P

MESH = pl.DeviceIdType.MESH
F32 = jnp.float32
BF16 = jnp.bfloat16
GELU_ROOT = 0.7978845608028654
GELU_CUBE = 0.044715
TILES = 2


def gelu_and_slope(value):
    square = value * value
    bent = jnp.tanh(GELU_ROOT * value * (1.0 + GELU_CUBE * square))
    rise = 0.5 * (1.0 + bent)
    slope = rise + 0.5 * value * (1.0 - bent * bent) * (
        GELU_ROOT * (1.0 + 3.0 * GELU_CUBE * square)
    )
    return value * rise, slope


def dot(left, right, left_dim, right_dim):
    return lax.dot_general(
        left, right, (((left_dim,), (right_dim,)), ((), ())), preferred_element_type=F32
    )


def flat_rows(blocks):
    return blocks.astype(F32).reshape(-1, blocks.shape[-1]).astype(BF16)


class Copies:
    def __init__(self, send, recv):
        self.send, self.recv, self.used = send, recv, 0

    def start(self, source, landing, device):
        copy = pltpu.make_async_remote_copy(
            src_ref=source,
            dst_ref=landing,
            send_sem=self.send.at[self.used],
            recv_sem=self.recv.at[self.used],
            device_id=(device,),
            device_id_type=MESH,
        )
        self.used += 1
        copy.start()
        return copy


def wait_all(copies):
    for copy in copies:
        copy.wait()


def step_kernel(
    size,
    plane,
    score_scale,
    facts,
    query_features,
    passage_features,
    own_code,
    base_pos,
    units,
    w_first,
    w_second,
    out_loss,
    out_first,
    out_second,
    unit_land,
    feat_base,
    feat_tail,
    q_base,
    q_tail,
    p_base,
    p_tail,
    pos_land,
    all_q,
    all_p,
    scores,
    stat_land,
    dq_own_base,
    dq_own_tail,
    dq_out_base,
    dq_out_tail,
    dq_land_base,
    dq_land_tail,
    dp_own_base,
    dp_own_tail,
    dp_out_base,
    dp_out_tail,
    dp_land_base,
    dp_land_tail,
    loss_land,
    de_base,
    de_tail,
    all_x,
    own,
    outgoing,
    landing,
    sums,
    forward,
    landed,
    send_sems,
    recv_sems,
    line_send,
    line_recv,
):
    me = lax.axis_index("dp")
    rows = size // plane
    half = rows // 2
    lanes = plane // 2
    stride = size // 16
    row = lax.div(me, plane)
    spot = lax.rem(me, plane)
    core = lax.rem(me, 2)
    lane = lax.div(spot, 2)
    column = spot - core
    place = lax.div(me, stride)
    partner = me + 1 - 2 * core
    width, hidden_width = w_first.shape
    embed = w_second.shape[1]
    base = q_base.shape[1]
    unit = q_tail.shape[1]
    hidden_half = hidden_width // 2
    tile = hidden_half // TILES
    per_tile = half // TILES
    chunk = hidden_half // (half * lanes * 2)
    copies = Copies(send_sems, recv_sems)

    plane_peers = [row * plane + lax.rem(spot + k, plane) for k in range(1, plane)]
    line_peers = [lax.rem(row + k, rows) * plane + spot for k in range(1, rows)]
    barrier = pltpu.get_barrier_semaphore()

    def greet(device):
        pl.semaphore_signal(barrier, inc=1, device_id=(device,), device_id_type=MESH)

    for k in range(1, 16):
        greet(lax.rem(place + k, 16) * stride + lax.rem(me, stride))
    for device in plane_peers:
        greet(device)
    in_column = 2 * row + core
    for k in range(1, 2 * rows):
        other = lax.rem(in_column + k, 2 * rows)
        greet(plane * lax.div(other, 2) + column + lax.rem(other, 2))
    pl.semaphore_wait(barrier, 15 + plane - 1 + 2 * rows - 1)

    unit_copies = []
    for k in range(1, 16):
        wrap = lax.div(place + k, 16)
        there = place + k - 16 * wrap
        unit_copies.append(
            copies.start(
                units.at[there - 1 + wrap],
                unit_land.at[place],
                there * stride + lax.rem(me, stride),
            )
        )

    def tower(features):
        total = None
        for low in range(0, hidden_width, tile):
            act = dot(features, w_first[:, low : low + tile], 1, 0)
            hidden = gelu_and_slope(act)[0].astype(BF16)
            part = dot(hidden, w_second[low : low + tile, :], 1, 0)
            total = part if total is None else total + part
        return total.astype(BF16)

    feat_base[core, 0] = query_features[:base]
    feat_base[core, 1] = passage_features[:base]
    pair_x = [copies.start(feat_base.at[core], feat_base.at[core], partner)]
    embedded = tower(feat_base[core].reshape(2 * base, width))
    q_base[spot] = embedded[:base]
    p_base[row] = embedded[base:]
    q_copies = [copies.start(q_base.at[spot], q_base.at[spot], device) for device in plane_peers]
    p_copies = [copies.start(p_base.at[row], p_base.at[row], device) for device in line_peers]

    wait_all(unit_copies)
    heavy = facts[0, 1] == 1
    got = unit_land[facts[0, 0]].astype(F32)
    tail_q = jnp.where(heavy, query_features[base : base + unit].astype(F32), got[:, :width])
    tail_p = jnp.where(
        heavy, passage_features[base : base + unit].astype(F32), got[:, width : 2 * width]
    )
    code = jnp.where(heavy, own_code[...].astype(F32), got[:, 2 * width :])
    tail_pos = code[:, :1] * 256.0 + code[:, 1:2]
    tail_x = jnp.concatenate([tail_q, tail_p], axis=0)
    feat_tail[core] = tail_x.reshape(2, unit, width).astype(BF16)
    tail_e = tower(tail_x.astype(BF16)).astype(F32)
    q_tail[spot] = tail_e[:unit].astype(BF16)
    p_tail[row] = tail_e[unit:].astype(BF16)
    pos_land[spot, 0] = base_pos[...]
    sub = lax.broadcasted_iota(jnp.int32, (unit, base), 0) + spot * unit
    along = lax.broadcasted_iota(jnp.int32, (unit, base), 1)
    pos_land[spot, 1] = jnp.sum(jnp.where(sub == along, tail_pos, 0.0), axis=0, keepdims=True)
    for device in plane_peers:
        q_copies.append(copies.start(pos_land.at[spot], pos_land.at[spot], device))
        q_copies.append(copies.start(q_tail.at[spot], q_tail.at[spot], device))
    for device in line_peers:
        p_copies.append(copies.start(p_tail.at[row], p_tail.at[row], device))
    pair_x.append(copies.start(feat_tail.at[core], feat_tail.at[core], partner))
    wait_all(q_copies)
    wait_all(p_copies)

    q_rows, p_rows = plane * base, rows * base
    all_q[:q_rows] = q_base[...].reshape(q_rows, embed)
    all_q[q_rows:] = flat_rows(q_tail[...])
    all_p[:p_rows] = p_base[...].reshape(p_rows, embed)
    all_p[p_rows:] = flat_rows(p_tail[...])
    pos_tail = pos_land[0, 1]
    for k in range(1, plane):
        pos_tail = pos_tail + pos_land[k, 1]
    wanted = jnp.concatenate(
        [pos_land[k, 0] for k in range(plane)] + [pos_tail[:, : plane * unit]], axis=1
    )
    ids = jnp.concatenate(
        [lax.broadcasted_iota(jnp.int32, (base, 1), 0) + facts[1, k] for k in range(rows)]
        + [lax.broadcasted_iota(jnp.int32, (unit, 1), 0) + facts[2, k] for k in range(rows)],
        axis=0,
    ).astype(F32)
    scores[...] = score_scale * dot(all_p[...], all_q[...], 1, 1)
    value = scores[...]
    hit = ids == wanted
    top = jnp.max(value, axis=0, keepdims=True)
    stat_land[spot, 0:1] = top
    stat_land[spot, 1:2] = jnp.sum(jnp.exp(value - top), axis=0, keepdims=True)
    stat_land[spot, 2:3] = jnp.sum(jnp.where(hit, value, 0.0), axis=0, keepdims=True)
    stat_land[spot, 3:4] = jnp.zeros_like(top)
    wait_all(
        [copies.start(stat_land.at[spot], stat_land.at[spot], device) for device in plane_peers]
    )
    stats = stat_land[...]
    tops = stats[:, 0]
    row_top = jnp.max(tops, axis=0, keepdims=True)
    mass = jnp.sum(stats[:, 1] * jnp.exp(tops - row_top), axis=0, keepdims=True)
    log_norm = row_top + jnp.log(mass)
    found = jnp.sum(stats[:, 2], axis=0, keepdims=True)
    loss_land[row] = jnp.broadcast_to(
        jnp.sum(log_norm - found, axis=1, keepdims=True), loss_land.shape[1:]
    )
    grads_t = (jnp.exp(scores[...] - log_norm) - hit.astype(F32)).astype(BF16)

    def scatter(part, own_base, own_tail, out_base, out_tail, land_base, land_tail, mine, peers):
        split = own_base.shape[0] * base
        own_base[...] = part[:split].reshape(own_base.shape)
        own_tail[...] = part[split:].reshape(own_tail.shape)
        out_base[...] = own_base[...].astype(out_base.dtype)
        out_tail[...] = own_tail[...].astype(out_tail.dtype)
        made = []
        for there, device in peers:
            made.append(copies.start(out_base.at[there], land_base.at[mine], device))
            made.append(copies.start(out_tail.at[there], land_tail.at[mine], device))
        return made

    def gathered(own_part, land, mine, members):
        total = own_part[mine]
        for k in range(1, members):
            total = total + land[lax.rem(mine + k, members)].astype(F32)
        return total.astype(BF16)

    dq_copies = scatter(
        score_scale * dot(grads_t, all_p[...], 0, 0),
        dq_own_base,
        dq_own_tail,
        dq_out_base,
        dq_out_tail,
        dq_land_base,
        dq_land_tail,
        spot,
        [(lax.rem(spot + k, plane), plane_peers[k - 1]) for k in range(1, plane)],
    )
    dp_copies = scatter(
        score_scale * dot(grads_t, all_q[...], 1, 0),
        dp_own_base,
        dp_own_tail,
        dp_out_base,
        dp_out_tail,
        dp_land_base,
        dp_land_tail,
        row,
        [(lax.rem(row + k, rows), line_peers[k - 1]) for k in range(1, rows)],
    )
    loss_copies = [
        copies.start(loss_land.at[row], loss_land.at[row], device) for device in line_peers
    ]
    wait_all(pair_x)
    x_rows = 4 * base
    all_x[:x_rows] = feat_base[...].reshape(x_rows, width)
    all_x[x_rows:] = flat_rows(feat_tail[...])
    wait_all(dq_copies)
    de_base[core, 0] = gathered(dq_own_base, dq_land_base, spot, plane)
    de_tail[core, 0] = gathered(dq_own_tail, dq_land_tail, spot, plane)
    wait_all(dp_copies)
    de_base[core, 1] = gathered(dp_own_base, dp_land_base, row, rows)
    de_tail[core, 1] = gathered(dp_own_tail, dp_land_tail, row, rows)
    pair_de = [
        copies.start(de_base.at[core], de_base.at[core], partner),
        copies.start(de_tail.at[core], de_tail.at[core], partner),
    ]
    wait_all(loss_copies)
    loss = loss_land[0]
    for k in range(1, rows):
        loss = loss + loss_land[k]
    out_loss[...] = loss

    lane_copies = []
    for t in range(TILES):
        start = pl.multiple_of(core * hidden_half + t * tile, 128)
        act = dot(all_x[...], w_first[:, pl.ds(start, tile)], 1, 0)
        hidden, slope = gelu_and_slope(act)
        hidden = hidden.astype(BF16)
        if t == 0:
            wait_all(pair_de)
        de = jnp.concatenate(
            [de_base[...].reshape(x_rows, embed), flat_rows(de_tail[...])], axis=0
        )
        back = dot(de, w_second[pl.ds(start, tile), :], 1, 1)
        act_grad = (slope * back).astype(BF16)
        first = dot(act_grad, all_x[...], 0, 0)
        second = dot(hidden, de, 0, 0)
        for i in range(per_tile):
            for m in range(lanes):
                for j in range(2):
                    at = ((i * lanes + m) * 2 + j) * chunk
                    for part, low in ((first, 0), (second, width)):
                        high = low + part.shape[1]
                        piece = part[at : at + chunk]
                        own[t * per_tile + i, m, j, :, low:high] = piece
                        outgoing[t * per_tile + i, m, j, :, low:high] = piece.astype(BF16)
        made = []
        for k in range(1, lanes):
            there = lax.rem(lane + k, lanes)
            made.append(
                copies.start(
                    outgoing.at[pl.ds(t * per_tile, per_tile), there],
                    landing.at[lane, pl.ds(t * per_tile, per_tile)],
                    plane * row + 2 * there + core,
                )
            )
        lane_copies.append(made)

    sender_core = lax.div(row, half)

    def line_copy(i, j):
        return pltpu.make_async_remote_copy(
            src_ref=forward.at[i, j],
            dst_ref=landed.at[row],
            send_sem=line_send.at[i, j],
            recv_sem=line_recv.at[row],
            device_id=(plane * (half * core + i) + column + j,),
            device_id_type=MESH,
        )

    for t in range(TILES):
        wait_all(lane_copies[t])
        for i in range(t * per_tile, (t + 1) * per_tile):
            for j in range(2):
                total = own[i, lane, j]
                for k in range(1, lanes):
                    total = total + landing[lax.rem(lane + k, lanes), i, j].astype(F32)
                sums[i, j] = total
                forward[i, j] = total.astype(BF16)

                @pl.when(plane * (half * core + i) + column + j != me)
                def _():
                    line_copy(i, j).start()

    for i in range(half):
        for j in range(2):

            @pl.when(plane * (half * core + i) + column + j != me)
            def _():
                line_copy(i, j).wait_send()

    for sender_row in range(rows):
        sender = plane * sender_row + column + sender_core

        @pl.when(sender != me)
        def _():
            pltpu.make_async_remote_copy(
                src_ref=forward.at[0, 0],
                dst_ref=landed.at[sender_row],
                send_sem=line_send.at[0, 0],
                recv_sem=line_recv.at[sender_row],
                device_id=(sender,),
                device_id_type=MESH,
            ).wait_recv()

    total = jnp.where(sender_core == core, sums[lax.rem(row, half), core], 0.0)
    for sender_row in range(rows):
        sender = plane * sender_row + column + sender_core
        total = total + jnp.where(sender == me, 0.0, landed[sender_row].astype(F32))
    out_first[...] = total[:, :width]
    out_second[...] = total[:, width:]


def step(size, plane, score_scale, facts, *arrays):
    query_features, _, _, base_pos, units, w_first, w_second = arrays
    rows, lanes = size // plane, plane // 2
    half = rows // 2
    width, hidden_width = w_first.shape
    embed = w_second.shape[1]
    chunk = hidden_width // size
    across = width + embed
    base, unit = base_pos.shape[1], units.shape[1]
    block = base + unit
    vmem = pl.BlockSpec(memory_space=pltpu.VMEM)
    count = 15 + 4 * (plane - 1) + 2 * (rows - 1) + 2
    count += 2 * (plane - 1) + 3 * (rows - 1) + 2 + TILES * (lanes - 1)

    def split(members, dtype):
        return [
            pltpu.VMEM((members, base, embed), dtype),
            pltpu.VMEM((members, unit, embed), dtype),
        ]

    scratch = [
        pltpu.VMEM((16,) + units.shape[1:], BF16),
        pltpu.VMEM((2, 2, base, width), BF16),
        pltpu.VMEM((2, 2, unit, width), BF16),
        *split(plane, BF16),
        *split(rows, BF16),
        pltpu.VMEM((plane, 2, 1, base), F32),
        pltpu.VMEM((plane * block, embed), BF16),
        pltpu.VMEM((rows * block, embed), BF16),
        pltpu.VMEM((rows * block, plane * block), F32),
        pltpu.VMEM((plane, 4, plane * block), F32),
        *split(plane, F32),
        *split(plane, BF16),
        *split(plane, BF16),
        *split(rows, F32),
        *split(rows, BF16),
        *split(rows, BF16),
        pltpu.VMEM((rows, 8, 128), F32),
        pltpu.VMEM((2, 2, base, embed), BF16),
        pltpu.VMEM((2, 2, unit, embed), BF16),
        pltpu.VMEM((4 * block, width), BF16),
        pltpu.VMEM((half, lanes, 2, chunk, across), F32),
        pltpu.VMEM((half, lanes, 2, chunk, across), BF16),
        pltpu.VMEM((lanes, half, 2, chunk, across), BF16),
        pltpu.VMEM((half, 2, chunk, across), F32),
        pltpu.VMEM((half, 2, chunk, across), BF16),
        pltpu.VMEM((rows, chunk, across), BF16),
        pltpu.SemaphoreType.DMA((count,)),
        pltpu.SemaphoreType.DMA((count,)),
        pltpu.SemaphoreType.DMA((half, 2)),
        pltpu.SemaphoreType.DMA((rows,)),
    ]
    return pl.pallas_call(
        functools.partial(step_kernel, size, plane, score_scale),
        out_shape=[
            jax.ShapeDtypeStruct((8, 128), F32),
            jax.ShapeDtypeStruct((chunk, width), F32),
            jax.ShapeDtypeStruct((chunk, embed), F32),
        ],
        in_specs=[pl.BlockSpec(memory_space=pltpu.SMEM)] + [vmem] * 7,
        out_specs=[vmem] * 3,
        scratch_shapes=scratch,
        compiler_params=pltpu.CompilerParams(
            collective_id=0, has_side_effects=True, vmem_limit_bytes=60 * 1024 * 1024
        ),
    )(facts, *arrays)


def body(query_features, passage_features, counts, positives, w_first, w_second):
    device_count = lax.axis_size("dp")
    plane = 1 << device_count.bit_length() // 2
    rows = device_count // plane
    my_index = lax.axis_index("dp")
    stride = device_count // 16
    base_rows = query_features.shape[0] // 2
    unit_rows = base_rows // 16
    block_rows = base_rows + unit_rows
    pair_count = block_rows * device_count
    score_scale = 2.5 * w_second.shape[1] ** (-0.5)

    devices = jnp.arange(device_count, dtype=jnp.int32)
    heavy_dev = (counts > base_rows).astype(jnp.int32)
    line = my_index % plane + plane * jnp.arange(rows, dtype=jnp.int32)
    asked = jnp.concatenate([my_index[None], line]).astype(jnp.int32)
    same_mat = (devices[None, :] % stride == asked[:, None] % stride) & (heavy_dev[None, :] == 1)
    source = jnp.sum(jnp.where(same_mat, devices[None, :], 0), axis=1)
    offset = jnp.sum(jnp.where(devices[None, :] < asked[:, None], counts[None, :], 0), axis=1)
    source_offset = jnp.sum(
        jnp.where(devices[None, :] < source[:, None], counts[None, :], 0), axis=1
    )
    piece = asked // stride - (source < asked).astype(jnp.int32)
    tail_offset = jnp.where(
        source == asked, offset + base_rows, source_offset + block_rows + piece * unit_rows
    )
    mine = jnp.stack([source[0] // stride, (source[0] == my_index).astype(jnp.int32)])
    facts = jnp.stack([jnp.pad(mine, (0, rows - 2)), offset[1:], tail_offset[1:]])

    lanes = jnp.arange(128, dtype=jnp.int32)
    spare = positives[base_rows:]
    coded = jnp.where(lanes[None, :] == 0, spare[:, None] // 256, spare[:, None] % 256)
    coded = jnp.where(lanes[None, :] < 2, coded, 0).astype(BF16)
    units = jnp.concatenate(
        [query_features[block_rows:], passage_features[block_rows:], coded[unit_rows:]], axis=1
    )
    units = units.reshape(15, unit_rows, units.shape[1])
    losses, total_first, total_second = step(
        device_count,
        plane,
        score_scale,
        facts,
        query_features,
        passage_features,
        coded[:unit_rows],
        positives[:base_rows].astype(F32)[None, :],
        units,
        w_first,
        w_second,
    )
    return (losses[0, 0] / pair_count, total_first.T, total_second)


def solution(mesh):
    return jax.shard_map(
        body,
        mesh=mesh,
        in_specs=(P("dp", None), P("dp", None), P(), P("dp"), P(), P()),
        out_specs=(P(), P(None, "dp"), P("dp", None)),
        check_vma=False,
    )
```

time: 408 us -> 93.3 us (0.23); the launches traced: 403 us -> 92.7 us
  waiting for transfers between devices: 205 us -> 0 us
  blocking collectives: 85.3 us -> 0 us
  Pallas kernels: 0 us -> 78.6 us
  local copies, waits for them, and re-layouts: 42.6 us -> 6.82 us
  matrix products: 34.8 us -> 0 us
  between operations: 17.2 us -> 2.67 us
  other arithmetic: 12.7 us -> 4.64 us
  starting transfers between devices: 5.57 us -> 0 us
    reduce_scatter x2 -> x0, waiting for transfers between devices: 196 us -> none  [the longest x1 113 us: body(): lax.psum_scatter(first_query + first_passage, 'dp', scatter_dimension=1,...]
    pallas_call x0 -> x1, Pallas kernels: none -> 78.6 us  [step(): pl.pallas_call(functools.partial(step_kernel, size, plane, score_scale),...]
    unnamed x1 -> x0, blocking collectives: 45.3 us -> none
    all_gather x1 -> x0, blocking collectives: 40.1 us -> none  [body(): all_pos = lax.all_gather(positives, 'dp', axis=0, tiled=True)]
    dot_general x11 -> x0, matrix products: 34.8 us -> none  [the longest x2 11.9 us: weight_terms(): lax.dot_general(features, pre_grad, (((0,), (0,)), ((), ())), preferred_e...]
    gather x5 -> x0, local copies, waits for them, and re-layouts: 33.8 us -> none  [the longest x1 32.5 us: body(): anchor = jnp.take(all_pos, slot_grid)]
    ppermute x4 -> x0, waiting for transfers between devices: 8.89 us -> none  [from_partner(): return lax.ppermute(block, axis, route)]
    ppermute x4 -> x0, starting transfers between devices: 5.22 us -> none  [from_partner(): return lax.ppermute(block, axis, route)]
  transfers between devices with their start and end apart: 8 -> 0, of which waited for: 5 -> 0; matrix products, arithmetic and copies ran while one was open for 16% -> 0% of each run, Pallas kernels for 0% -> 0%
where the time goes in v3:
time: 93.3 us; the launch traced here: 92.7 us
  Pallas kernels  78.6 us (84%)
  local copies, waits for them, and re-layouts  6.82 us (7%)
  other arithmetic  4.64 us (5%)
  between operations  2.67 us (3%)
    pallas_call x1, Pallas kernels, step(): pl.pallas_call(functools.partial(step_kernel, size, plane, score_scale),...  78.6 us
    unnamed x2, local copies, waits for them, and re-layouts  3.1 us

profile of v3, /device:TPU:9, one launch (start us, length us, event | category | flops | bytes accessed | tf_op | source)
XLA Modules:
  0.0 92.7 jit_solution(12027072908956955057)
XLA Ops:
  0.7 0.7 fusion
  1.3 0.1 and_select_fusion.3
  1.4 0.2 select_reduce_fusion.2
  1.8 0.1 pad_add_fusion.2
  1.9 0.9 select_reduce_fusion.1
  2.8 0.1 slice_bitcast_fusion
  2.8 0.6 pad_add_fusion.facts
  3.4 1.3 %and_select_fusion.1 = (s32[128]{0:T(128)S(1)}, s32[128]{0:T(128)S(1)}, f32[1,128]{1,0:T(1,128)}) fusion(s32[256]{0:T(256)} %param.9), kind=kLoop, calls=%fused_computation.9 | loop fusion | flops 2048 | bytes 2560 | tf_op jit(solution)/shard_map/jit(floor_divide)/jit(_where)/select_n | solution.py:502
  4.7 0.1 select_convert_fusion
  4.8 0.6 slice.41.own_code
  5.4 0.9 %slice.37 = bf16[120,768]{1,0:T(8,128)(2,1)S(1)} slice(bf16[256,768]{1,0:T(8,128)(2,1)} %query_features.1), slice={[136:256], [0:768]} | slice | bytes 368640 | tf_op jit(solution)/shard_map/slice | solution.py:505
  6.3 0.9 %slice.38 = bf16[120,768]{1,0:T(8,128)(2,1)S(1)} slice(bf16[256,768]{1,0:T(8,128)(2,1)} %passage_features.1), slice={[136:256], [0:768]} | slice | bytes 368640 | tf_op jit(solution)/shard_map/slice | solution.py:505
  7.3 0.8 maximum_bitcast_fusion.units
  8.1 78.6 %shard_map.85 = (f32[8,128]{1,0:T(8,128)}, f32[48,768]{1,0:T(8,128)}, f32[48,384]{1,0:T(8,128)}) custom-call(s32[3,4]{1,0:T(4,128)} %pad_add_fusion.facts, bf16[256,768]{1,0:T(8,128)(2,1)} %query_features.1, bf16[256,768]{1,0:T(8,128)(2,1)} %passage_features.1, bf16[8,128]{1,0:T(8,128)(2,1)} %slice.41.own_code, f32[1,128]{1,0:T(1,128)} %get-tuple-element.15.base_pos, ...), custom_call_target="tpu_custom_call" | custom-call | tf_op jit(solution)/shard_map/pallas_call | solution.py:455
  86.6 1.2 %slice.40 = f32[1,1]{1,0:T(1,128)} slice(f32[8,128]{1,0:T(8,128)} %get-tuple-element.6), slice={[0:1], [0:1]} | slice | bytes 8 | tf_op jit(solution)/shard_map/slice | solution.py:521
  88.5 1.6 %copy.11 = f32[768,48]{0,1:T(8,128)} copy(f32[768,48]{0,1:T(8,128)} %bitcast.17) | data formatting | bytes 294912
  90.0 1.5 %copy.12 = f32[48,384]{1,0:T(8,128)} copy(f32[48,384]{1,0:T(8,128)} %get-tuple-element.25) | data formatting | bytes 147456
  (7 shorter events, 0.0 us)

commit v4 on v3

--- a/solution.py
+++ b/solution.py
@@ -62,18 +62,17 @@
     size,
     plane,
     score_scale,
-    facts,
+    counts,
     query_features,
     passage_features,
-    own_code,
-    base_pos,
-    units,
+    positives,
     w_first,
     w_second,
     out_loss,
-    out_first,
-    out_second,
+    out_all,
+    units,
     unit_land,
+    unit_pos,
     feat_base,
     feat_tail,
     q_base,
@@ -151,6 +150,11 @@
         greet(plane * lax.div(other, 2) + column + lax.rem(other, 2))
     pl.semaphore_wait(barrier, 15 + plane - 1 + 2 * rows - 1)
 
+    spare = base + unit
+    units[:, :, :width] = query_features[spare:].astype(F32).reshape(15, unit, width).astype(BF16)
+    units[:, :, width:] = passage_features[spare:].astype(F32).reshape(15, unit, width).astype(BF16)
+    unit_pos[place] = positives[...].astype(F32)
+
     unit_copies = []
     for k in range(1, 16):
         wrap = lax.div(place + k, 16)
@@ -162,6 +166,34 @@
                 there * stride + lax.rem(me, stride),
             )
         )
+        unit_copies.append(
+            copies.start(
+                unit_pos.at[place], unit_pos.at[place], there * stride + lax.rem(me, stride)
+            )
+        )
+
+    heavies = []
+    for g in range(stride):
+        at = jnp.int32(0)
+        for k in range(16):
+            at = at + jnp.where(counts[g + stride * k] > base, g + stride * k, 0)
+        heavies.append(at)
+    source = jnp.int32(0)
+    for g in range(stride):
+        source = source + jnp.where(lax.rem(me, stride) == g, heavies[g], 0)
+    heavy_place = jnp.int32(0)
+    for k in range(16):
+        heavy_place = heavy_place + jnp.where(source >= stride * (k + 1), 1, 0)
+
+    def offset_of(device):
+        before = jnp.int32(0)
+        for at in heavies:
+            before = before + jnp.where(at < device, 1, 0)
+        return base * (device + before)
+
+    def tail_row(device):
+        piece = lax.div(device, stride) - jnp.where(source < device, 1, 0)
+        return jnp.where(source == device, base, spare + unit * piece)
 
     def tower(features):
         total = None
@@ -182,20 +214,21 @@
     p_copies = [copies.start(p_base.at[row], p_base.at[row], device) for device in line_peers]
 
     wait_all(unit_copies)
-    heavy = facts[0, 1] == 1
-    got = unit_land[facts[0, 0]].astype(F32)
-    tail_q = jnp.where(heavy, query_features[base : base + unit].astype(F32), got[:, :width])
-    tail_p = jnp.where(
-        heavy, passage_features[base : base + unit].astype(F32), got[:, width : 2 * width]
-    )
-    code = jnp.where(heavy, own_code[...].astype(F32), got[:, 2 * width :])
-    tail_pos = code[:, :1] * 256.0 + code[:, 1:2]
+    heavy = source == me
+    got = unit_land[heavy_place].astype(F32)
+    tail_q = jnp.where(heavy, query_features[base:spare].astype(F32), got[:, :width])
+    tail_p = jnp.where(heavy, passage_features[base:spare].astype(F32), got[:, width:])
+    slots = lax.broadcasted_iota(jnp.int32, (unit, positives.shape[1]), 1)
+    chosen = lax.broadcasted_iota(jnp.int32, slots.shape, 0) + tail_row(me)
+    tail_pos = jnp.sum(
+        jnp.where(slots == chosen, unit_pos[heavy_place], 0.0), axis=1, keepdims=True
+    )
     tail_x = jnp.concatenate([tail_q, tail_p], axis=0)
     feat_tail[core] = tail_x.reshape(2, unit, width).astype(BF16)
     tail_e = tower(tail_x.astype(BF16)).astype(F32)
     q_tail[spot] = tail_e[:unit].astype(BF16)
     p_tail[row] = tail_e[unit:].astype(BF16)
-    pos_land[spot, 0] = base_pos[...]
+    pos_land[spot, 0] = positives[:, :base].astype(F32)
     sub = lax.broadcasted_iota(jnp.int32, (unit, base), 0) + spot * unit
     along = lax.broadcasted_iota(jnp.int32, (unit, base), 1)
     pos_land[spot, 1] = jnp.sum(jnp.where(sub == along, tail_pos, 0.0), axis=0, keepdims=True)
@@ -219,9 +252,13 @@
     wanted = jnp.concatenate(
         [pos_land[k, 0] for k in range(plane)] + [pos_tail[:, : plane * unit]], axis=1
     )
+    line = [plane * k + spot for k in range(rows)]
     ids = jnp.concatenate(
-        [lax.broadcasted_iota(jnp.int32, (base, 1), 0) + facts[1, k] for k in range(rows)]
-        + [lax.broadcasted_iota(jnp.int32, (unit, 1), 0) + facts[2, k] for k in range(rows)],
+        [lax.broadcasted_iota(jnp.int32, (base, 1), 0) + offset_of(device) for device in line]
+        + [
+            lax.broadcasted_iota(jnp.int32, (unit, 1), 0) + offset_of(source) + tail_row(device)
+            for device in line
+        ],
         axis=0,
     ).astype(F32)
     scores[...] = score_scale * dot(all_p[...], all_q[...], 1, 1)
@@ -307,7 +344,7 @@
     loss = loss_land[0]
     for k in range(1, rows):
         loss = loss + loss_land[k]
-    out_loss[...] = loss
+    out_loss[...] = loss * (1.0 / (size * spare))
 
     lane_copies = []
     for t in range(TILES):
@@ -396,22 +433,44 @@
     for sender_row in range(rows):
         sender = plane * sender_row + column + sender_core
         total = total + jnp.where(sender == me, 0.0, landed[sender_row].astype(F32))
-    out_first[...] = total[:, :width]
-    out_second[...] = total[:, width:]
-
-
-def step(size, plane, score_scale, facts, *arrays):
-    query_features, _, _, base_pos, units, w_first, w_second = arrays
+    out_all[...] = total
+
+
+def split_kernel(loss, total, mean_loss, first, second):
+    width = first.shape[1]
+    mean_loss[0] = loss[0, 0]
+    first[...] = total[:, :width]
+    second[...] = total[:, width:]
+
+
+def split_outputs(loss, total, width):
+    vmem = pl.BlockSpec(memory_space=pltpu.VMEM)
+    chunk, across = total.shape
+    return pl.pallas_call(
+        split_kernel,
+        out_shape=[
+            jax.ShapeDtypeStruct((1,), F32),
+            jax.ShapeDtypeStruct((chunk, width), F32),
+            jax.ShapeDtypeStruct((chunk, across - width), F32),
+        ],
+        in_specs=[pl.BlockSpec(memory_space=pltpu.SMEM), vmem],
+        out_specs=[pl.BlockSpec(memory_space=pltpu.SMEM), vmem, vmem],
+    )(loss, total)
+
+
+def step(size, plane, score_scale, counts, *arrays):
+    query_features, _, positives, w_first, w_second = arrays
     rows, lanes = size // plane, plane // 2
     half = rows // 2
     width, hidden_width = w_first.shape
     embed = w_second.shape[1]
     chunk = hidden_width // size
     across = width + embed
-    base, unit = base_pos.shape[1], units.shape[1]
+    base = query_features.shape[0] // 2
+    unit = base // 16
     block = base + unit
     vmem = pl.BlockSpec(memory_space=pltpu.VMEM)
-    count = 15 + 4 * (plane - 1) + 2 * (rows - 1) + 2
+    count = 30 + 4 * (plane - 1) + 2 * (rows - 1) + 2
     count += 2 * (plane - 1) + 3 * (rows - 1) + 2 + TILES * (lanes - 1)
 
     def split(members, dtype):
@@ -421,7 +480,9 @@
         ]
 
     scratch = [
-        pltpu.VMEM((16,) + units.shape[1:], BF16),
+        pltpu.VMEM((15, unit, 2 * width), BF16),
+        pltpu.VMEM((16, unit, 2 * width), BF16),
+        pltpu.VMEM((16,) + positives.shape, F32),
         pltpu.VMEM((2, 2, base, width), BF16),
         pltpu.VMEM((2, 2, unit, width), BF16),
         *split(plane, BF16),
@@ -456,69 +517,34 @@
         functools.partial(step_kernel, size, plane, score_scale),
         out_shape=[
             jax.ShapeDtypeStruct((8, 128), F32),
-            jax.ShapeDtypeStruct((chunk, width), F32),
-            jax.ShapeDtypeStruct((chunk, embed), F32),
+            jax.ShapeDtypeStruct((chunk, across), F32),
         ],
-        in_specs=[pl.BlockSpec(memory_space=pltpu.SMEM)] + [vmem] * 7,
-        out_specs=[vmem] * 3,
+        in_specs=[pl.BlockSpec(memory_space=pltpu.SMEM)] + [vmem] * 5,
+        out_specs=[vmem] * 2,
         scratch_shapes=scratch,
         compiler_params=pltpu.CompilerParams(
             collective_id=0, has_side_effects=True, vmem_limit_bytes=60 * 1024 * 1024
         ),
-    )(facts, *arrays)
+    )(counts, *arrays)
 
 
 def body(query_features, passage_features, counts, positives, w_first, w_second):
     device_count = lax.axis_size("dp")
     plane = 1 << device_count.bit_length() // 2
-    rows = device_count // plane
-    my_index = lax.axis_index("dp")
-    stride = device_count // 16
-    base_rows = query_features.shape[0] // 2
-    unit_rows = base_rows // 16
-    block_rows = base_rows + unit_rows
-    pair_count = block_rows * device_count
     score_scale = 2.5 * w_second.shape[1] ** (-0.5)
-
-    devices = jnp.arange(device_count, dtype=jnp.int32)
-    heavy_dev = (counts > base_rows).astype(jnp.int32)
-    line = my_index % plane + plane * jnp.arange(rows, dtype=jnp.int32)
-    asked = jnp.concatenate([my_index[None], line]).astype(jnp.int32)
-    same_mat = (devices[None, :] % stride == asked[:, None] % stride) & (heavy_dev[None, :] == 1)
-    source = jnp.sum(jnp.where(same_mat, devices[None, :], 0), axis=1)
-    offset = jnp.sum(jnp.where(devices[None, :] < asked[:, None], counts[None, :], 0), axis=1)
-    source_offset = jnp.sum(
-        jnp.where(devices[None, :] < source[:, None], counts[None, :], 0), axis=1
-    )
-    piece = asked // stride - (source < asked).astype(jnp.int32)
-    tail_offset = jnp.where(
-        source == asked, offset + base_rows, source_offset + block_rows + piece * unit_rows
-    )
-    mine = jnp.stack([source[0] // stride, (source[0] == my_index).astype(jnp.int32)])
-    facts = jnp.stack([jnp.pad(mine, (0, rows - 2)), offset[1:], tail_offset[1:]])
-
-    lanes = jnp.arange(128, dtype=jnp.int32)
-    spare = positives[base_rows:]
-    coded = jnp.where(lanes[None, :] == 0, spare[:, None] // 256, spare[:, None] % 256)
-    coded = jnp.where(lanes[None, :] < 2, coded, 0).astype(BF16)
-    units = jnp.concatenate(
-        [query_features[block_rows:], passage_features[block_rows:], coded[unit_rows:]], axis=1
-    )
-    units = units.reshape(15, unit_rows, units.shape[1])
-    losses, total_first, total_second = step(
+    loss, total = step(
         device_count,
         plane,
         score_scale,
-        facts,
+        counts,
         query_features,
         passage_features,
-        coded[:unit_rows],
-        positives[:base_rows].astype(F32)[None, :],
-        units,
+        positives[None, :],
         w_first,
         w_second,
     )
-    return (losses[0, 0] / pair_count, total_first.T, total_second)
+    mean_loss, grad_first, grad_second = split_outputs(loss, total, w_first.shape[0])
+    return (mean_loss[0], grad_first.T, grad_second)
 
 
 def solution(mesh):

time: 93.3 us -> 81.2 us (0.87)
  local copies, waits for them, and re-layouts: 6.82 us -> 0 us
  other arithmetic: 4.64 us -> 0 us
  between operations: 2.67 us -> 0.64 us
  Pallas kernels: 78.6 us -> 80.1 us
    slice x5 -> x0, local copies, waits for them, and re-layouts: 3.64 us -> none  [the longest x1 1.19 us: body(): return (losses[0, 0] / pair_count, total_first.T, total_second)]
    unnamed x2 -> x0, local copies, waits for them, and re-layouts: 3.1 us -> none
    pallas_call x0 -> x1, Pallas kernels: none -> 1.65 us  [split_outputs(): pl.pallas_call(split_kernel, out_shape=[jax.ShapeDtypeStruct((1,), F32),...]
    select_n x5 -> x0, other arithmetic: 1.37 us -> none  [the longest x1 1.27 us: body(): spare[:, None] // 256]
    reduce_sum x2 -> x0, other arithmetic: 1.05 us -> none  [the longest x1 0.87 us: body(): jnp.sum(jnp.where(devices[None, :] < asked[:, None], counts[None, :], 0),...]
where the time goes in v4:
time: 81.2 us; the launch traced here: 80.7 us
  Pallas kernels  80.1 us (99%)
    pallas_call x1, Pallas kernels, step(): pl.pallas_call(functools.partial(step_kernel, size, plane, score_scale),...  78.5 us
    pallas_call x1, Pallas kernels, split_outputs(): pl.pallas_call(split_kernel, out_shape=[jax.ShapeDtypeStruct((1,), F32),...  1.65 us

profile of v4, /device:TPU:9, one launch (start us, length us, event | category | flops | bytes accessed | tf_op | source)
XLA Modules:
  0.0 80.7 jit_solution(6481039271125749389)
XLA Ops:
  0.6 78.5 %shard_map.85 = (f32[8,128]{1,0:T(8,128)}, f32[48,1152]{1,0:T(8,128)}) custom-call(s32[32]{0:T(128)} %counts.1, bf16[256,768]{1,0:T(8,128)(2,1)} %query_features.1, bf16[256,768]{1,0:T(8,128)(2,1)} %passage_features.1, s32[1,256]{1,0:T(1,128)} %bitcast.3, bf16[768,1536]{1,0:T(8,128)(2,1)} %w_first.1, bf16[1536,384]{1,0:T(8,128)(2,1)} %w_second.1), custom_call_target="tpu_custom_call" | custom-call | tf_op jit(solution)/shard_map/pallas_call | solution.py:516
  79.1 1.6 %shard_map.86 = (f32[1]{0:T(128)}, f32[48,768]{1,0:T(8,128)}, f32[48,384]{1,0:T(8,128)}) custom-call(f32[8,128]{1,0:T(8,128)} %get-tuple-element.8.loss, f32[48,1152]{1,0:T(8,128)} %get-tuple-element.9.total), custom_call_target="tpu_custom_call" | custom-call | tf_op jit(solution)/shard_map/pallas_call | solution.py:449

commit v5 on v4

--- a/solution.py
+++ b/solution.py
@@ -66,11 +66,13 @@
     query_features,
     passage_features,
     positives,
-    w_first,
-    w_second,
+    w_first_hbm,
+    w_second_hbm,
     out_loss,
     out_all,
     units,
+    unit_mid,
+    unit_pass,
     unit_land,
     unit_pos,
     feat_base,
@@ -110,8 +112,19 @@
     recv_sems,
     line_send,
     line_recv,
+    w_first,
+    w_second,
+    all_hidden,
+    all_slope,
+    load_sems,
 ):
     me = lax.axis_index("dp")
+    loads = [
+        pltpu.make_async_copy(w_first_hbm, w_first, load_sems.at[0]),
+        pltpu.make_async_copy(w_second_hbm, w_second, load_sems.at[1]),
+    ]
+    for load in loads:
+        load.start()
     rows = size // plane
     half = rows // 2
     lanes = plane // 2
@@ -151,26 +164,30 @@
     pl.semaphore_wait(barrier, 15 + plane - 1 + 2 * rows - 1)
 
     spare = base + unit
-    units[:, :, :width] = query_features[spare:].astype(F32).reshape(15, unit, width).astype(BF16)
-    units[:, :, width:] = passage_features[spare:].astype(F32).reshape(15, unit, width).astype(BF16)
+    near = plane // stride
+    aside = lax.div(spot, stride)
+    extra_q = query_features[spare:].astype(F32).reshape(15, unit, width).astype(BF16)
+    extra_p = passage_features[spare:].astype(F32).reshape(15, unit, width).astype(BF16)
+    for u in range(15):
+        there = u + lax.div(u + 16 - place, 16)
+        units[lax.div(there, near), lax.rem(there, near), :, :width] = extra_q[u]
+        units[lax.div(there, near), lax.rem(there, near), :, width:] = extra_p[u]
     unit_pos[place] = positives[...].astype(F32)
 
+    mid_copies = []
+    for k in range(1, near):
+        there = lax.rem(aside + k, near)
+        mid_copies.append(
+            copies.start(
+                units.at[:, there],
+                unit_mid.at[aside],
+                row * plane + there * stride + lax.rem(me, stride),
+            )
+        )
     unit_copies = []
     for k in range(1, 16):
-        wrap = lax.div(place + k, 16)
-        there = place + k - 16 * wrap
-        unit_copies.append(
-            copies.start(
-                units.at[there - 1 + wrap],
-                unit_land.at[place],
-                there * stride + lax.rem(me, stride),
-            )
-        )
-        unit_copies.append(
-            copies.start(
-                unit_pos.at[place], unit_pos.at[place], there * stride + lax.rem(me, stride)
-            )
-        )
+        device = lax.rem(place + k, 16) * stride + lax.rem(me, stride)
+        unit_copies.append(copies.start(unit_pos.at[place], unit_pos.at[place], device))
 
     heavies = []
     for g in range(stride):
@@ -207,15 +224,28 @@
     feat_base[core, 0] = query_features[:base]
     feat_base[core, 1] = passage_features[:base]
     pair_x = [copies.start(feat_base.at[core], feat_base.at[core], partner)]
+    wait_all(loads)
     embedded = tower(feat_base[core].reshape(2 * base, width))
     q_base[spot] = embedded[:base]
     p_base[row] = embedded[base:]
     q_copies = [copies.start(q_base.at[spot], q_base.at[spot], device) for device in plane_peers]
+    wait_all(mid_copies)
+    source_row, source_aside = jnp.int32(0), heavy_place
+    for k in range(1, rows):
+        beyond = heavy_place >= k * near
+        source_row = source_row + jnp.where(beyond, 1, 0)
+        source_aside = source_aside - jnp.where(beyond, near, 0)
+    unit_pass[...] = jnp.where(source_aside == aside, units[:, aside], unit_mid[source_aside])
+    for k in range(1, rows):
+        there = lax.rem(row + k, rows)
+        unit_copies.append(
+            copies.start(unit_pass.at[there], unit_land.at[row], there * plane + spot)
+        )
     p_copies = [copies.start(p_base.at[row], p_base.at[row], device) for device in line_peers]
 
     wait_all(unit_copies)
     heavy = source == me
-    got = unit_land[heavy_place].astype(F32)
+    got = jnp.where(source_row == row, unit_pass[row], unit_land[source_row]).astype(F32)
     tail_q = jnp.where(heavy, query_features[base:spare].astype(F32), got[:, :width])
     tail_p = jnp.where(heavy, passage_features[base:spare].astype(F32), got[:, width:])
     slots = lax.broadcasted_iota(jnp.int32, (unit, positives.shape[1]), 1)
@@ -330,6 +360,11 @@
     x_rows = 4 * base
     all_x[:x_rows] = feat_base[...].reshape(x_rows, width)
     all_x[x_rows:] = flat_rows(feat_tail[...])
+    for t in range(TILES):
+        start = pl.multiple_of(core * hidden_half + t * tile, 128)
+        hidden, slope = gelu_and_slope(dot(all_x[...], w_first[:, pl.ds(start, tile)], 1, 0))
+        all_hidden[t] = hidden.astype(BF16)
+        all_slope[t] = slope
     wait_all(dq_copies)
     de_base[core, 0] = gathered(dq_own_base, dq_land_base, spot, plane)
     de_tail[core, 0] = gathered(dq_own_tail, dq_land_tail, spot, plane)
@@ -349,18 +384,15 @@
     lane_copies = []
     for t in range(TILES):
         start = pl.multiple_of(core * hidden_half + t * tile, 128)
-        act = dot(all_x[...], w_first[:, pl.ds(start, tile)], 1, 0)
-        hidden, slope = gelu_and_slope(act)
-        hidden = hidden.astype(BF16)
         if t == 0:
             wait_all(pair_de)
         de = jnp.concatenate(
             [de_base[...].reshape(x_rows, embed), flat_rows(de_tail[...])], axis=0
         )
         back = dot(de, w_second[pl.ds(start, tile), :], 1, 1)
-        act_grad = (slope * back).astype(BF16)
+        act_grad = (all_slope[t] * back).astype(BF16)
         first = dot(act_grad, all_x[...], 0, 0)
-        second = dot(hidden, de, 0, 0)
+        second = dot(all_hidden[t], de, 0, 0)
         for i in range(per_tile):
             for m in range(lanes):
                 for j in range(2):
@@ -480,8 +512,10 @@
         ]
 
     scratch = [
-        pltpu.VMEM((15, unit, 2 * width), BF16),
-        pltpu.VMEM((16, unit, 2 * width), BF16),
+        pltpu.VMEM((rows, 16 // rows, unit, 2 * width), BF16),
+        pltpu.VMEM((16 // rows, rows, unit, 2 * width), BF16),
+        pltpu.VMEM((rows, unit, 2 * width), BF16),
+        pltpu.VMEM((rows, unit, 2 * width), BF16),
         pltpu.VMEM((16,) + positives.shape, F32),
         pltpu.VMEM((2, 2, base, width), BF16),
         pltpu.VMEM((2, 2, unit, width), BF16),
@@ -512,6 +546,11 @@
         pltpu.SemaphoreType.DMA((count,)),
         pltpu.SemaphoreType.DMA((half, 2)),
         pltpu.SemaphoreType.DMA((rows,)),
+        pltpu.VMEM(w_first.shape, BF16),
+        pltpu.VMEM(w_second.shape, BF16),
+        pltpu.VMEM((TILES, 4 * block, hidden_width // 2 // TILES), BF16),
+        pltpu.VMEM((TILES, 4 * block, hidden_width // 2 // TILES), F32),
+        pltpu.SemaphoreType.DMA((2,)),
     ]
     return pl.pallas_call(
         functools.partial(step_kernel, size, plane, score_scale),
@@ -519,7 +558,8 @@
             jax.ShapeDtypeStruct((8, 128), F32),
             jax.ShapeDtypeStruct((chunk, across), F32),
         ],
-        in_specs=[pl.BlockSpec(memory_space=pltpu.SMEM)] + [vmem] * 5,
+        in_specs=[pl.BlockSpec(memory_space=pltpu.SMEM)] + [vmem] * 3
+        + [pl.BlockSpec(memory_space=pl.ANY)] * 2,
         out_specs=[vmem] * 2,
         scratch_shapes=scratch,
         compiler_params=pltpu.CompilerParams(

time: 81.2 us -> 78.7 us (0.969)
  Pallas kernels: 80.1 us -> 77.8 us
    pallas_call x1, Pallas kernels: 78.5 us -> 76.2 us  [step(): pl.pallas_call(functools.partial(step_kernel, size, plane, score_scale),...]
where the time goes in v5:
time: 78.7 us; the launch traced here: 78.5 us
  Pallas kernels  77.8 us (99%)
    pallas_call x1, Pallas kernels, step(): pl.pallas_call(functools.partial(step_kernel, size, plane, score_scale),...  76.2 us
    pallas_call x1, Pallas kernels, split_outputs(): pl.pallas_call(split_kernel, out_shape=[jax.ShapeDtypeStruct((1,), F32),...  1.65 us

profile of v5, /device:TPU:9, one launch (start us, length us, event | category | flops | bytes accessed | tf_op | source)
XLA Modules:
  0.0 78.5 jit_solution(6690928776168304555)
XLA Ops:
  0.6 76.2 %shard_map.85 = (f32[8,128]{1,0:T(8,128)}, f32[48,1152]{1,0:T(8,128)}) custom-call(s32[32]{0:T(128)} %counts.1, bf16[256,768]{1,0:T(8,128)(2,1)} %query_features.1, bf16[256,768]{1,0:T(8,128)(2,1)} %passage_features.1, s32[1,256]{1,0:T(1,128)} %bitcast.3, bf16[768,1536]{1,0:T(8,128)(2,1)} %w_first_hbm.1, bf16[1536,384]{1,0:T(8,128)(2,1)} %w_second_hbm.1), custom_call_target="tpu_custom_call" | custom-call | tf_op jit(solution)/shard_map/pallas_call | solution.py:555
  76.8 1.6 %shard_map.86 = (f32[1]{0:T(128)}, f32[48,768]{1,0:T(8,128)}, f32[48,384]{1,0:T(8,128)}) custom-call(f32[8,128]{1,0:T(8,128)} %get-tuple-element.8.loss, f32[48,1152]{1,0:T(8,128)} %get-tuple-element.9.total), custom_call_target="tpu_custom_call" | custom-call | tf_op jit(solution)/shard_map/pallas_call | solution.py:481

commit v6 on v5

--- a/solution.py
+++ b/solution.py
@@ -161,7 +161,6 @@
     for k in range(1, 2 * rows):
         other = lax.rem(in_column + k, 2 * rows)
         greet(plane * lax.div(other, 2) + column + lax.rem(other, 2))
-    pl.semaphore_wait(barrier, 15 + plane - 1 + 2 * rows - 1)
 
     spare = base + unit
     near = plane // stride
@@ -173,6 +172,8 @@
         units[lax.div(there, near), lax.rem(there, near), :, :width] = extra_q[u]
         units[lax.div(there, near), lax.rem(there, near), :, width:] = extra_p[u]
     unit_pos[place] = positives[...].astype(F32)
+
+    pl.semaphore_wait(barrier, 15 + plane - 1 + 2 * rows - 1)
 
     mid_copies = []
     for k in range(1, near):
@@ -381,38 +382,38 @@
         loss = loss + loss_land[k]
     out_loss[...] = loss * (1.0 / (size * spare))
 
-    lane_copies = []
-    for t in range(TILES):
-        start = pl.multiple_of(core * hidden_half + t * tile, 128)
-        if t == 0:
-            wait_all(pair_de)
-        de = jnp.concatenate(
-            [de_base[...].reshape(x_rows, embed), flat_rows(de_tail[...])], axis=0
-        )
-        back = dot(de, w_second[pl.ds(start, tile), :], 1, 1)
-        act_grad = (all_slope[t] * back).astype(BF16)
-        first = dot(act_grad, all_x[...], 0, 0)
-        second = dot(all_hidden[t], de, 0, 0)
+    def keep(t, part, low):
+        high = low + part.shape[1]
         for i in range(per_tile):
             for m in range(lanes):
                 for j in range(2):
                     at = ((i * lanes + m) * 2 + j) * chunk
-                    for part, low in ((first, 0), (second, width)):
-                        high = low + part.shape[1]
-                        piece = part[at : at + chunk]
-                        own[t * per_tile + i, m, j, :, low:high] = piece
-                        outgoing[t * per_tile + i, m, j, :, low:high] = piece.astype(BF16)
+                    piece = part[at : at + chunk]
+                    own[t * per_tile + i, m, j, :, low:high] = piece
+                    outgoing[t * per_tile + i, m, j, :, low:high] = piece.astype(BF16)
         made = []
+        block = pl.ds(t * per_tile, per_tile)
         for k in range(1, lanes):
             there = lax.rem(lane + k, lanes)
             made.append(
                 copies.start(
-                    outgoing.at[pl.ds(t * per_tile, per_tile), there],
-                    landing.at[lane, pl.ds(t * per_tile, per_tile)],
+                    outgoing.at[block, there, :, :, pl.ds(low, high - low)],
+                    landing.at[lane, block, :, :, pl.ds(low, high - low)],
                     plane * row + 2 * there + core,
                 )
             )
-        lane_copies.append(made)
+        return made
+
+    wait_all(pair_de)
+    de = jnp.concatenate([de_base[...].reshape(x_rows, embed), flat_rows(de_tail[...])], axis=0)
+    lane_copies = [keep(0, dot(all_hidden[0], de, 0, 0), width)]
+    for t in range(TILES):
+        start = pl.multiple_of(core * hidden_half + t * tile, 128)
+        back = dot(de, w_second[pl.ds(start, tile), :], 1, 1)
+        act_grad = (all_slope[t] * back).astype(BF16)
+        lane_copies[t] += keep(t, dot(act_grad, all_x[...], 0, 0), 0)
+        if t + 1 < TILES:
+            lane_copies.append(keep(t + 1, dot(all_hidden[t + 1], de, 0, 0), width))
 
     sender_core = lax.div(row, half)
 
@@ -503,7 +504,7 @@
     block = base + unit
     vmem = pl.BlockSpec(memory_space=pltpu.VMEM)
     count = 30 + 4 * (plane - 1) + 2 * (rows - 1) + 2
-    count += 2 * (plane - 1) + 3 * (rows - 1) + 2 + TILES * (lanes - 1)
+    count += 2 * (plane - 1) + 3 * (rows - 1) + 2 + 2 * TILES * (lanes - 1)
 
     def split(members, dtype):
         return [

time: 78.7 us -> 77.8 us (0.989)
  Pallas kernels: 77.8 us -> 77 us
    pallas_call x1, Pallas kernels: 76.2 us -> 75.4 us  [step(): pl.pallas_call(functools.partial(step_kernel, size, plane, score_scale),...]
where the time goes in v6:
time: 77.8 us; the launch traced here: 77.6 us
  Pallas kernels  77 us (99%)
    pallas_call x1, Pallas kernels, step(): pl.pallas_call(functools.partial(step_kernel, size, plane, score_scale),...  75.4 us
    pallas_call x1, Pallas kernels, split_outputs(): pl.pallas_call(split_kernel, out_shape=[jax.ShapeDtypeStruct((1,), F32),...  1.65 us

profile of v6, /device:TPU:9, one launch (start us, length us, event | category | flops | bytes accessed | tf_op | source)
XLA Modules:
  0.0 77.6 jit_solution(11614942272734351358)
XLA Ops:
  0.6 75.4 %shard_map.85 = (f32[8,128]{1,0:T(8,128)}, f32[48,1152]{1,0:T(8,128)}) custom-call(s32[32]{0:T(128)} %counts.1, bf16[256,768]{1,0:T(8,128)(2,1)} %query_features.1, bf16[256,768]{1,0:T(8,128)(2,1)} %passage_features.1, s32[1,256]{1,0:T(1,128)} %bitcast.3, bf16[768,1536]{1,0:T(8,128)(2,1)} %w_first_hbm.1, bf16[1536,384]{1,0:T(8,128)(2,1)} %w_second_hbm.1), custom_call_target="tpu_custom_call" | custom-call | tf_op jit(solution)/shard_map/pallas_call | solution.py:556
  76.0 1.6 %shard_map.86 = (f32[1]{0:T(128)}, f32[48,768]{1,0:T(8,128)}, f32[48,384]{1,0:T(8,128)}) custom-call(f32[8,128]{1,0:T(8,128)} %get-tuple-element.8.loss, f32[48,1152]{1,0:T(8,128)} %get-tuple-element.9.total), custom_call_target="tpu_custom_call" | custom-call | tf_op jit(solution)/shard_map/pallas_call | solution.py:482

commit v7 on v6

--- a/solution.py
+++ b/solution.py
@@ -369,13 +369,18 @@
     wait_all(dq_copies)
     de_base[core, 0] = gathered(dq_own_base, dq_land_base, spot, plane)
     de_tail[core, 0] = gathered(dq_own_tail, dq_land_tail, spot, plane)
+
+    def send_de(side):
+        return [
+            copies.start(de_base.at[core, side], de_base.at[core, side], partner),
+            copies.start(de_tail.at[core, side], de_tail.at[core, side], partner),
+        ]
+
+    pair_de = send_de(0)
     wait_all(dp_copies)
     de_base[core, 1] = gathered(dp_own_base, dp_land_base, row, rows)
     de_tail[core, 1] = gathered(dp_own_tail, dp_land_tail, row, rows)
-    pair_de = [
-        copies.start(de_base.at[core], de_base.at[core], partner),
-        copies.start(de_tail.at[core], de_tail.at[core], partner),
-    ]
+    pair_de += send_de(1)
     wait_all(loss_copies)
     loss = loss_land[0]
     for k in range(1, rows):
@@ -504,7 +509,7 @@
     block = base + unit
     vmem = pl.BlockSpec(memory_space=pltpu.VMEM)
     count = 30 + 4 * (plane - 1) + 2 * (rows - 1) + 2
-    count += 2 * (plane - 1) + 3 * (rows - 1) + 2 + 2 * TILES * (lanes - 1)
+    count += 2 * (plane - 1) + 3 * (rows - 1) + 4 + 2 * TILES * (lanes - 1)
 
     def split(members, dtype):
         return [

time: 77.8 us -> 77.7 us (level)
  no operation moved by 1% of the time
where the time goes in v7:
time: 77.7 us; the launch traced here: 77.5 us
  Pallas kernels  76.9 us (99%)
    pallas_call x1, Pallas kernels, step(): pl.pallas_call(functools.partial(step_kernel, size, plane, score_scale),...  75.2 us
    pallas_call x1, Pallas kernels, split_outputs(): pl.pallas_call(split_kernel, out_shape=[jax.ShapeDtypeStruct((1,), F32),...  1.65 us

profile of v7, /device:TPU:9, one launch (start us, length us, event | category | flops | bytes accessed | tf_op | source)
XLA Modules:
  0.0 77.5 jit_solution(8161651718557706192)
XLA Ops:
  0.6 75.2 %shard_map.85 = (f32[8,128]{1,0:T(8,128)}, f32[48,1152]{1,0:T(8,128)}) custom-call(s32[32]{0:T(128)} %counts.1, bf16[256,768]{1,0:T(8,128)(2,1)} %query_features.1, bf16[256,768]{1,0:T(8,128)(2,1)} %passage_features.1, s32[1,256]{1,0:T(1,128)} %bitcast.3, bf16[768,1536]{1,0:T(8,128)(2,1)} %w_first_hbm.1, bf16[1536,384]{1,0:T(8,128)(2,1)} %w_second_hbm.1), custom_call_target="tpu_custom_call" | custom-call | tf_op jit(solution)/shard_map/pallas_call | solution.py:561
  75.9 1.6 %shard_map.86 = (f32[1]{0:T(128)}, f32[48,768]{1,0:T(8,128)}, f32[48,384]{1,0:T(8,128)}) custom-call(f32[8,128]{1,0:T(8,128)} %get-tuple-element.8.loss, f32[48,1152]{1,0:T(8,128)} %get-tuple-element.9.total), custom_call_target="tpu_custom_call" | custom-call | tf_op jit(solution)/shard_map/pallas_call | solution.py:487
